TPU v7x, 8 devices: a whole 2x2x1 slice. The times are simulated.
8 devices in a mesh: batch: 1 (over z), row: 2 (over y), col: 4 (over x, core).
Axes of the slice: x: 2, y: 2, z: 1, core: 2. Of those that a mesh axis runs over, the one named last changes fastest.
Arguments:
- l_mat: bfloat16 [8192, 8192], P(('batch', 'row'), 'col')
- b_mat: bfloat16 [8192, 16384], P(('batch', 'row'), 'col')
Outputs:
- output: bfloat16 [8192, 16384], P(('batch', 'row'), 'col')
All inputs are finite; a program needn't handle non-finite values.
Results may differ from a plain program's by a relative error of at most 0.001.
Values are sent between devices in bfloat16 or wider.
A program may use at most 1 GiB of HBM per device.

v0:
```python
import functools

import jax
import jax.numpy as jnp
import numpy as np
from jax import lax
from jax.experimental import pallas as pl
from jax.experimental.pallas import tpu as pltpu
from jax.sharding import PartitionSpec as P


TM = 1024
KB = 1024
NBUF = 6
FIELDS = 6
WIDTHS = (512, 1024, 1024, 512, 512)
FIRST = (384, 640)
TAIL = (2048, 1024, 512, 512)
SPLIT = 2
KEEP = 1024
DOT = functools.partial(jnp.dot, preferred_element_type=jnp.float32)


def plan(half, with_off):
    tables, nb = [], half // KB
    for row in range(2):
        start = row * nb
        steps, seen = [], set()
        for r in range(half // TM):
            ks = list(range(0 if with_off else start, start + -(-(r + 1) * TM // KB)))
            for k in ks:
                slot = k if with_off else k - start
                steps.append((r, k, int(k == ks[0]), int(k == ks[-1]), int(k not in seen), slot))
                seen.add(k)
        tables.append(steps)
    counts = tuple(len(s) for s in tables)
    flat = np.zeros((2, max(counts), FIELDS), np.int32)
    for row in range(2):
        flat[row, :counts[row]] = tables[row]
    return counts, jnp.asarray(flat.reshape(-1))


def chunk_kernel(half, depth, src0, dst0, width, counts, cuts, n_alias, tab, info, l0, l1, l2, l3, b_loc, *rest):
    pieces = rest[:len(cuts)]
    rest = rest[len(cuts) + n_alias:]
    off = bool(cuts)
    if off:
        out, bv, lv, acc, ov, lsem, bsem, osem = rest
    else:
        out, keep, bv, lv, acc, lsem, bsem, ksem = rest
    row, col = info[0], info[1]
    stride = max(counts) * FIELDS
    n = jnp.where(row == 0, counts[0], counts[1])
    per, nb = depth // KB, half // KB

    def field(t, f):
        return tab[row * stride + t * FIELDS + f]

    def l_start(t, slot):
        r, k = field(t, 0), field(t, 1)
        which = lax.bitwise_xor(k // per, col)
        for i, ref in enumerate((l0, l1, l2, l3)):
            @pl.when(which == i)
            def _():
                pltpu.make_async_copy(
                    ref.at[pl.ds(r * TM, TM), pl.ds(lax.rem(k, per) * KB, KB)],
                    lv.at[slot], lsem.at[slot]).start()

    def b_local(k, slot):
        return pltpu.make_async_copy(
            b_loc.at[pl.ds(k * KB, KB), pl.ds(src0, width)], bv.at[pl.ds(slot * KB, KB), :], bsem.at[slot])

    def b_recv_start(k):
        for ref, cut in zip(pieces, cuts):
            lo, hi = max(k * KB, cut), min((k + 1) * KB, cut + ref.shape[0])
            if lo < hi:
                pltpu.make_async_copy(
                    ref.at[pl.ds(lo - cut, hi - lo), :], bv.at[pl.ds(lo, hi - lo), :], bsem.at[k]).start()

    def o_copy(r, slot):
        return pltpu.make_async_copy(
            ov.at[slot], out.at[pl.ds(r * TM, TM), pl.ds(dst0, width)], osem.at[slot])

    def keep_copy(ref):
        return pltpu.make_async_copy(ref.at[:, pl.ds((half - KEEP) % depth, KEEP)], keep, ksem)

    for k in range(nb):
        if off:
            @pl.when(row == 0)
            def _():
                b_local(k, k).start()

            @pl.when(row == 1)
            def _():
                b_recv_start(k)
        else:
            b_local(k, k).start()
        l_start(k, k)
    if off:
        for k in range(nb):
            @pl.when(row == 1)
            def _():
                b_local(k, nb + k).start()
    for t in range(nb, NBUF - 1):
        l_start(t, t)
    if not off:
        kept = lax.bitwise_xor((half - KEEP) // depth, col)
        for i, ref in enumerate((l0, l1, l2, l3)):
            @pl.when((row == 1) & (kept == i))
            def _():
                keep_copy(ref).start()

    def step(t, _):
        slot = lax.rem(t, NBUF)
        r, at = field(t, 0), field(t, 5)

        @pl.when(t + NBUF - 1 < n)
        def _():
            l_start(t + NBUF - 1, lax.rem(t + NBUF - 1, NBUF))

        @pl.when(field(t, 4) == 1)
        def _():
            b_local(0, at).wait()

        pltpu.make_async_copy(l0.at[pl.ds(0, TM), pl.ds(0, KB)], lv.at[slot], lsem.at[slot]).wait()
        rows_k = pl.ds(pl.multiple_of(at * KB, KB), KB)
        first = field(t, 2)

        @pl.when(first == 1)
        def _():
            acc[...] = DOT(lv[slot], bv[rows_k, :])

        @pl.when(first == 0)
        def _():
            acc[...] += DOT(lv[slot], bv[rows_k, :])

        @pl.when(field(t, 3) == 1)
        def _():
            if off:
                oslot = lax.rem(r, 2)

                @pl.when(r >= 2)
                def _():
                    o_copy(r - 2, oslot).wait()

                ov[oslot] = acc[...].astype(ov.dtype)
                o_copy(r, oslot).start()
            else:
                out[pl.ds(pl.multiple_of(r * TM, TM), TM), :] = acc[...]

        return 0

    lax.fori_loop(0, n, step, 0)
    if off:
        last = half // TM
        o_copy(last - 2, (last - 2) % 2).wait()
        o_copy(last - 1, (last - 1) % 2).wait()
    else:
        @pl.when(row == 1)
        def _():
            keep_copy(l0).wait()


def tail_kernel(half, depth, k0, kw, src0, dst0, width, final, info, part, piece, *rest):
    row, col = info[0], info[1]
    tiles = half // TM
    kept = k0 >= half - KEEP
    if final:
        keep, (out, ov, osem) = rest[0], rest[-3:]
    elif kept:
        keep, out = rest
    else:
        l_refs, (out, bv, lv, lsem, bsem) = rest[:4], rest[4:]
    which = lax.bitwise_xor(k0 // depth, col)

    def l_copy(ref, t):
        slot = lax.rem(t, 2)
        return pltpu.make_async_copy(
            ref.at[pl.ds(t * TM, TM), pl.ds(k0 % depth, kw)], lv.at[slot], lsem.at[slot])

    def l_start(t):
        for i, ref in enumerate(l_refs):
            @pl.when(which == i)
            def _():
                l_copy(ref, t).start()

    def o_copy(t):
        return pltpu.make_async_copy(
            ov.at[t], out.at[pl.ds(t * TM, TM), pl.ds(dst0, width)], osem.at[t])

    def put(t, rows, total):
        if final:
            ov[t] = total.astype(ov.dtype)
            o_copy(t).start()
        else:
            out[rows, :] = total

    @pl.when(row == 1)
    def _():
        if not kept:
            b_copy = pltpu.make_async_copy(piece, bv, bsem)
            b_copy.start()
            l_start(0)
            l_start(1)
            b_copy.wait()
        right = piece if kept else bv

        def add(t, _):
            rows = pl.ds(pl.multiple_of(t * TM, TM), TM)
            if kept:
                tile = keep[rows, pl.ds(k0 - (half - KEEP), kw)]
            else:
                l_copy(l_refs[0], t).wait()
                tile = lv[lax.rem(t, 2)]
            put(t, rows, part[rows, pl.ds(src0, width)] + DOT(tile, right[...]))
            if not kept:
                @pl.when(t + 2 < tiles)
                def _():
                    l_start(t + 2)
            return 0

        lax.fori_loop(0, tiles, add, 0, unroll=kept)

    @pl.when(row == 0)
    def _():
        def move(t, _):
            rows = pl.ds(pl.multiple_of(t * TM, TM), TM)
            put(t, rows, part[rows, pl.ds(src0, width)])
            return 0

        lax.fori_loop(0, tiles, move, 0)

    if final:
        for t in range(tiles):
            o_copy(t).wait()


def solution(mesh):
    block_spec = P(('batch', 'row'), 'col')
    x_swap = [(0, 2), (1, 3), (2, 0), (3, 1)]
    core_swap = [(0, 1), (1, 0), (2, 3), (3, 2)]
    n_first = len(FIRST) + 1
    hbm = pl.BlockSpec(memory_space=pltpu.HBM)
    vmem = pl.BlockSpec(memory_space=pltpu.VMEM)
    smem = pl.BlockSpec(memory_space=pltpu.SMEM)

    def in_hbm(array):
        return pltpu.with_memory_space_constraint(array, pltpu.HBM)

    def product(l_block, b_block):
        half, depth = l_block.shape
        dtype = b_block.dtype
        off_counts, off_tab = plan(half, True)
        diag_counts, diag_tab = plan(half, False)
        info = jnp.stack([lax.axis_index('row'), lax.axis_index('col')]).astype(jnp.int32)
        starts = np.cumsum((0,) + WIDTHS).tolist()
        tail0, tail_w = starts[-1], b_block.shape[1] - starts[-1]

        cuts0 = np.cumsum((0,) + FIRST).tolist()
        boxes = [(r, e - r, 0, WIDTHS[0]) for r, e in zip(cuts0, cuts0[1:] + [half])]
        boxes += [(0, half, c, w) for c, w in zip(starts[1:], WIDTHS[1:])]
        n_main = len(boxes)
        ends = np.cumsum(TAIL).tolist()
        boxes += [(e - h, h, tail0, tail_w) for e, h in zip(ends[:-1], TAIL)]
        last_w = tail_w // SPLIT
        boxes += [(half - TAIL[-1], TAIL[-1], tail0 + i * last_w, last_w) for i in range(SPLIT)]
        recv, source = [], b_block

        def send(j, source):
            r, h, c, w = boxes[j]
            piece = source[r:r + h, c:c + w]
            piece, source = lax.optimization_barrier((piece, source))
            recv.append(lax.ppermute(piece, 'row', [(0, 1), (1, 0)] if j == 0 else [(0, 1)]))
            return source

        n_early = len(boxes) - SPLIT - 1
        for j in range(n_early):
            source = send(j, source)
        lx = lax.ppermute(l_block, 'col', x_swap)
        lc = lax.ppermute(l_block, 'col', core_swap)
        lxc = lax.ppermute(lx, 'col', core_swap)
        l_refs = [l_block, lc, lx, lxc]

        def chunk(pieces, cuts, x, src0, dst0, width, counts, tab):
            alias = [] if x is None else [x]
            operands = [tab, info, *map(in_hbm, [*l_refs, b_block, *pieces]), *alias]
            scratch = [
                pltpu.VMEM(((2 if cuts else 1) * half, width), dtype),
                pltpu.VMEM((NBUF, TM, KB), dtype),
                pltpu.VMEM((TM, width), jnp.float32),
            ]
            sems = [pltpu.SemaphoreType.DMA((NBUF,)), pltpu.SemaphoreType.DMA((2 * half // KB,))]
            if cuts:
                out, out_spec = jax.ShapeDtypeStruct(b_block.shape, dtype), hbm
                scratch += [pltpu.VMEM((2, TM, width), dtype), *sems, pltpu.SemaphoreType.DMA((2,))]
            else:
                out = (pltpu.VMEM((half, width), jnp.float32), pltpu.VMEM((half, KEEP), dtype))
                out_spec = (vmem, vmem)
                scratch += [*sems, pltpu.SemaphoreType.DMA]
            limit = 2 * (NBUF * TM * KB + (2 if cuts else 1) * half * width + 6 * TM * width) + 2 * 2**20
            return pl.pallas_call(
                functools.partial(chunk_kernel, half, depth, src0, dst0, width, counts, cuts, len(alias)),
                out_shape=out,
                in_specs=[smem, smem] + [hbm] * (len(operands) - 2), out_specs=out_spec,
                scratch_shapes=scratch,
                input_output_aliases={len(operands) - 1: 0} if alias else {},
                compiler_params=pltpu.CompilerParams(vmem_limit_bytes=limit),
                cost_estimate=pl.CostEstimate(flops=max(counts) * 2 * TM * KB * width,
                                              bytes_accessed=max(counts) * 2 * TM * KB, transcendentals=0),
            )(*operands)

        def tail(keep, piece, part, x, k0, kw, src0, width):
            final, kept = x is not None, k0 >= half - KEEP
            operands = [info, part, pltpu.with_memory_space_constraint(piece, pltpu.VMEM) if kept else in_hbm(piece)]
            operands += [keep] if kept else list(map(in_hbm, l_refs))
            specs = [smem, vmem] + ([vmem, vmem] if kept else [hbm] * 5)
            scratch, need = [], 4 * TM * width + 2 * 2**20
            if final:
                operands.append(x)
                specs.append(hbm)
                out, out_spec = jax.ShapeDtypeStruct(x.shape, x.dtype), hbm
                scratch = [pltpu.VMEM((half // TM, TM, width), dtype), pltpu.SemaphoreType.DMA((half // TM,))]
                need += 2 * half * width
            else:
                out, out_spec = pltpu.VMEM(part.shape, part.dtype), vmem
                if not kept:
                    scratch = [pltpu.VMEM((kw, width), dtype), pltpu.VMEM((2, TM, kw), dtype),
                               pltpu.SemaphoreType.DMA((2,)), pltpu.SemaphoreType.DMA]
                    need += 2 * kw * (width + 2 * TM)
            return pl.pallas_call(
                functools.partial(tail_kernel, half, depth, k0, kw, src0, tail0 + src0, width, final),
                out_shape=out,
                in_specs=specs, out_specs=out_spec,
                scratch_shapes=scratch,
                input_output_aliases={len(operands) - 1: 0} if final else {1: 0},
                compiler_params=pltpu.CompilerParams(vmem_limit_bytes=need),
                cost_estimate=pl.CostEstimate(flops=2 * half * kw * width,
                                              bytes_accessed=2 * half * kw, transcendentals=0),
            )(*operands)

        x, part = None, None
        for j, width in enumerate(WIDTHS):
            if j == len(WIDTHS) - 1:
                x, b_block = lax.optimization_barrier((x, b_block))
                source = b_block
                for i in range(n_early, len(boxes)):
                    source = send(i, source)
                part, keep = chunk([], (), None, tail0, 0, tail_w, diag_counts, diag_tab)
                x, part, keep = lax.optimization_barrier((x, part, keep))
            pieces, cuts = (recv[:n_first], tuple(cuts0)) if j == 0 else ([recv[n_first - 1 + j]], (0,))
            x = chunk(pieces, cuts, x, starts[j], starts[j], width, off_counts, off_tab)
        x, part = lax.optimization_barrier((x, part))
        for j, (piece, (k0, kw, c, w)) in enumerate(zip(recv[n_main:], boxes[n_main:])):
            final = j >= len(TAIL) - 1
            done = tail(keep, piece, part, x if final else None, k0, kw, c - tail0, w)
            part, x = (part, done) if final else (done, x)
        return x

    return jax.shard_map(product, mesh=mesh, in_specs=(block_spec, block_spec), out_specs=block_spec, check_vma=False)
```

profile of v0, /device:TPU:0, one launch (start us, length us, event | category | flops | bytes accessed | tf_op | source)
XLA Modules:
  0.0 1111.8 jit_solution(16052984957725908731)
XLA Ops:
  0.0 3.3 collective-permute-start.1
  3.3 360.5 %collective-permute-done.1.l2.rest_2_ = bf16[4096,2048]{1,0:T(8,128)(2,1)} collective-permute-done((bf16[4096,2048]{1,0:T(8,128)(2,1)}, bf16[4096,2048]{1,0:T(8,128)(2,1)}, u32[]{:S(2)}, u32[]{:S(2)}) %collective-permute-start.1) | collective-permute-done | bytes 16777248 | tf_op jit(solution)/shard_map/ppermute | solution.py:279
  366.0 2.1 slice.38
  368.1 7.6 slice.39
  375.7 6.9 collective-permute-start.5
  382.6 2.9 collective-permute-start.8
  385.5 250.3 %collective-permute-done.6.rest_0_ = bf16[384,512]{1,0:T(8,128)(2,1)S(1)} collective-permute-done((bf16[384,512]{1,0:T(8,128)(2,1)S(1)}, bf16[384,512]{1,0:T(8,128)(2,1)S(1)}, u32[]{:S(2)}, u32[]{:S(2)}) %collective-permute-start.6) | collective-permute-done | bytes 393248 | tf_op jit(solution)/shard_map/ppermute | solution.py:273
  635.8 4.4 collective-permute-start.7
  640.2 7.6 slice.40
  647.8 6.1 collective-permute-done.7.rest_1_
  654.8 7.7 collective-permute-start.4
  662.5 4.4 slice.41
  666.9 4.5 slice.42
  671.4 3.1 slice.43
  674.4 2.3 slice.44
  676.8 3.3 collective-permute-start.3
  680.1 3.3 collective-permute-start.9
  683.4 2.6 collective-permute-start.10
  686.0 17.5 %shard_map.46.rest_1_ = bf16[4096,4096]{1,0:T(8,128)(2,1)} custom-call(s32[312]{0:T(512)S(1)} %copy-done, s32[2]{0:T(128)S(1)} %pad_add_fusion.info, bf16[4096,2048]{1,0:T(8,128)(2,1)} %rest_0_.3, bf16[4096,2048]{1,0:T(8,128)(2,1)} %collective-permute-done.l1.rest_1_, bf16[4096,2048]{1,0:T(8,128)(2,1)} %collective-permute-done.1.l2.rest_2_, ...), custom_call_target="tpu_custom_call" | custom-call | flops 27917287424 | bytes 54525952 | tf_op jit(solution)/shard_map/pallas_call | solution.py:301
  703.5 15.1 %collective-permute-start.11 = (bf16[1024,512]{1,0:T(8,128)(2,1)}, bf16[1024,512]{1,0:T(8,128)(2,1)}, u32[]{:S(2)}, u32[]{:S(2)}) collective-permute-start(bf16[1024,512]{1,0:T(8,128)(2,1)} %slice.44), channel_id=1, source_target_pairs={{0,4},{1,5},{2,6},{3,7}} | collective-permute-start | bytes 3145736 | tf_op jit(solution)/shard_map/ppermute | solution.py:273
  718.6 29.4 %shard_map.47.rest_1_ = bf16[4096,4096]{1,0:T(8,128)(2,1)} custom-call(s32[312]{0:T(512)S(1)} %copy-done, s32[2]{0:T(128)S(1)} %pad_add_fusion.info, bf16[4096,2048]{1,0:T(8,128)(2,1)} %rest_0_.3, bf16[4096,2048]{1,0:T(8,128)(2,1)} %collective-permute-done.l1.rest_1_, ...), custom_call_target="tpu_custom_call", output_to_operand_aliasing={{}: (8, {})} | custom-call | flops 55834574848 | bytes 54525952 | tf_op jit(solution)/shard_map/pallas_call | solution.py:301
  748.0 92.3 %collective-permute-done.4.rest_0_ = bf16[4096,1024]{1,0:T(8,128)(2,1)} collective-permute-done((bf16[4096,1024]{1,0:T(8,128)(2,1)}, bf16[4096,1024]{1,0:T(8,128)(2,1)}, u32[]{:S(2)}, u32[]{:S(2)}) %collective-permute-start.4) | collective-permute-done | bytes 8388640 | tf_op jit(solution)/shard_map/ppermute | solution.py:273
  840.3 29.4 %shard_map.48.rest_1_ = bf16[4096,4096]{1,0:T(8,128)(2,1)} custom-call(s32[312]{0:T(512)S(1)} %copy-done, s32[2]{0:T(128)S(1)} %pad_add_fusion.info, bf16[4096,2048]{1,0:T(8,128)(2,1)} %rest_0_.3, bf16[4096,2048]{1,0:T(8,128)(2,1)} %collective-permute-done.l1.rest_1_, ...), custom_call_target="tpu_custom_call", output_to_operand_aliasing={{}: (8, {})} | custom-call | flops 55834574848 | bytes 54525952 | tf_op jit(solution)/shard_map/pallas_call | solution.py:301
  869.8 60.4 %collective-permute-done.3.rest_0_ = bf16[4096,512]{1,0:T(8,128)(2,1)} collective-permute-done((bf16[4096,512]{1,0:T(8,128)(2,1)}, bf16[4096,512]{1,0:T(8,128)(2,1)}, u32[]{:S(2)}, u32[]{:S(2)}) %collective-permute-start.3) | collective-permute-done | bytes 4194336 | tf_op jit(solution)/shard_map/ppermute | solution.py:273
  930.2 17.5 %shard_map.49.rest_1_ = bf16[4096,4096]{1,0:T(8,128)(2,1)} custom-call(s32[312]{0:T(512)S(1)} %copy-done, s32[2]{0:T(128)S(1)} %pad_add_fusion.info, bf16[4096,2048]{1,0:T(8,128)(2,1)} %rest_0_.3, bf16[4096,2048]{1,0:T(8,128)(2,1)} %collective-permute-done.l1.rest_1_, ...), custom_call_target="tpu_custom_call", output_to_operand_aliasing={{}: (8, {})} | custom-call | flops 27917287424 | bytes 54525952 | tf_op jit(solution)/shard_map/pallas_call | solution.py:301
  947.7 17.8 %shard_map.50 = (f32[4096,512]{1,0:T(8,128)S(1)}, bf16[4096,1024]{1,0:T(8,128)(2,1)S(1)}) custom-call(s32[120]{0:T(128)S(1)} %copy-done.1, s32[2]{0:T(128)S(1)} %pad_add_fusion.info, bf16[4096,2048]{1,0:T(8,128)(2,1)} %rest_0_.3, bf16[4096,2048]{1,0:T(8,128)(2,1)} %collective-permute-done.l1.rest_1_, bf16[4096,2048]{1,0:T(8,128)(2,1)} %collective-permute-done.1.l2.rest_2_, ...), custom_call_target="tpu_custom_call" | custom-call | flops 10737418240 | bytes 20971520 | tf_op jit(solution)/shard_map/pallas_call | solution.py:301
  965.5 54.6 %collective-permute-done.9.rest_0_ = bf16[4096,512]{1,0:T(8,128)(2,1)} collective-permute-done((bf16[4096,512]{1,0:T(8,128)(2,1)}, bf16[4096,512]{1,0:T(8,128)(2,1)}, u32[]{:S(2)}, u32[]{:S(2)}) %collective-permute-start.9) | collective-permute-done | bytes 4194336 | tf_op jit(solution)/shard_map/ppermute | solution.py:273
  1020.1 17.5 %shard_map.51.rest_1_ = bf16[4096,4096]{1,0:T(8,128)(2,1)} custom-call(s32[312]{0:T(512)S(1)} %copy-done, s32[2]{0:T(128)S(1)} %pad_add_fusion.info, bf16[4096,2048]{1,0:T(8,128)(2,1)} %rest_0_.3, bf16[4096,2048]{1,0:T(8,128)(2,1)} %collective-permute-done.l1.rest_1_, ...), custom_call_target="tpu_custom_call", output_to_operand_aliasing={{}: (8, {})} | custom-call | flops 27917287424 | bytes 54525952 | tf_op jit(solution)/shard_map/pallas_call | solution.py:301
  1038.7 25.2 %collective-permute-start.12 = (bf16[512,512]{1,0:T(8,128)(2,1)S(1)}, bf16[512,512]{1,0:T(8,128)(2,1)S(1)}, u32[]{:S(2)}, u32[]{:S(2)}) collective-permute-start(bf16[512,512]{1,0:T(8,128)(2,1)S(1)} %slice.45), channel_id=1, source_target_pairs={{0,4},{1,5},{2,6},{3,7}} | collective-permute-start | bytes 1572872 | tf_op jit(solution)/shard_map/ppermute | solution.py:273
  1070.3 17.2 %collective-permute-done.11.piece = bf16[1024,512]{1,0:T(8,128)(2,1)} collective-permute-done((bf16[1024,512]{1,0:T(8,128)(2,1)}, bf16[1024,512]{1,0:T(8,128)(2,1)}, u32[]{:S(2)}, u32[]{:S(2)}) %collective-permute-start.11) | collective-permute-done | bytes 1048608 | tf_op jit(solution)/shard_map/ppermute | solution.py:273
  1089.2 9.5 collective-permute-done.12.piece
  1100.3 7.4 collective-permute-done.14.piece
  (30 shorter events, 17.8 us)
Async XLA Ops:
  0.0 363.8 %collective-permute-start.1 = (bf16[4096,2048]{1,0:T(8,128)(2,1)}, bf16[4096,2048]{1,0:T(8,128)(2,1)}, u32[]{:S(2)}, u32[]{:S(2)}) collective-permute-start(bf16[4096,2048]{1,0:T(8,128)(2,1)} %rest_0_.3), channel_id=1, source_target_pairs={{0,2},{1,3},{2,0},{3,1},{4,6},{5,7},{6,4},{7,5}} | collective-permute-start | bytes 50331656 | tf_op jit(solution)/shard_map/ppermute | solution.py:279
  3.3 676.8 %collective-permute-start = (bf16[4096,2048]{1,0:T(8,128)(2,1)}, bf16[4096,2048]{1,0:T(8,128)(2,1)}, u32[]{:S(2)}, u32[]{:S(2)}) collective-permute-start(bf16[4096,2048]{1,0:T(8,128)(2,1)} %rest_0_.3), channel_id=1, source_target_pairs={{0,1},{1,0},{2,3},{3,2},{4,5},{5,4},{6,7},{7,6}} | collective-permute-start | bytes 50331656 | tf_op jit(solution)/shard_map/ppermute | solution.py:280
  363.8 319.5 %collective-permute-start.2 = (bf16[4096,2048]{1,0:T(8,128)(2,1)}, bf16[4096,2048]{1,0:T(8,128)(2,1)}, u32[]{:S(2)}, u32[]{:S(2)}) collective-permute-start(bf16[4096,2048]{1,0:T(8,128)(2,1)} %collective-permute-done.1.l2.rest_2_), channel_id=1, source_target_pairs={{0,1},{1,0},{2,3},{3,2},{4,5},{5,4},{6,7},{7,6}} | collective-permute-start | bytes 50331656 | tf_op jit(solution)/shard_map/ppermute | solution.py:281
  375.7 327.8 %collective-permute-start.5 = (bf16[4096,1024]{1,0:T(8,128)(2,1)}, bf16[4096,1024]{1,0:T(8,128)(2,1)}, u32[]{:S(2)}, u32[]{:S(2)}) collective-permute-start(bf16[4096,1024]{1,0:T(8,128)(2,1)} %slice.39), channel_id=1, source_target_pairs={{0,4},{1,5},{2,6},{3,7}} | collective-permute-start | bytes 25165832 | tf_op jit(solution)/shard_map/ppermute | solution.py:273
  382.6 294.2 %collective-permute-start.8 = (bf16[3072,512]{1,0:T(8,128)(2,1)S(1)}, bf16[3072,512]{1,0:T(8,128)(2,1)}, u32[]{:S(2)}, u32[]{:S(2)}) collective-permute-start(bf16[3072,512]{1,0:T(8,128)(2,1)S(1)} %slice.38), channel_id=1, source_target_pairs={{0,4},{1,5},{2,6},{3,7}} | collective-permute-start | bytes 9437192 | tf_op jit(solution)/shard_map/ppermute | solution.py:273
  385.5 250.3 %collective-permute-start.6 = (bf16[384,512]{1,0:T(8,128)(2,1)S(1)}, bf16[384,512]{1,0:T(8,128)(2,1)S(1)}, u32[]{:S(2)}, u32[]{:S(2)}) collective-permute-start(bf16[384,512]{1,0:T(8,128)(2,1)S(1)} %slice.36), channel_id=1, source_target_pairs={{0,4},{4,0},{1,5},{5,1},{2,6},{6,2},{3,7},{7,3}} | collective-permute-start | bytes 1179656 | tf_op jit(solution)/shard_map/ppermute | solution.py:273
  635.8 12.0 %copy-start.3 = (bf16[384,512]{1,0:T(8,128)(2,1)}, bf16[384,512]{1,0:T(8,128)(2,1)S(1)}, u32[]{:S(2)}) copy-start(bf16[384,512]{1,0:T(8,128)(2,1)S(1)} %collective-permute-done.6.rest_0_) | copy-start | bytes 1179652
  635.8 18.2 %collective-permute-start.7 = (bf16[640,512]{1,0:T(8,128)(2,1)S(1)}, bf16[640,512]{1,0:T(8,128)(2,1)S(1)}, u32[]{:S(2)}, u32[]{:S(2)}) collective-permute-start(bf16[640,512]{1,0:T(8,128)(2,1)S(1)} %slice.37), channel_id=1, source_target_pairs={{0,4},{1,5},{2,6},{3,7}} | collective-permute-start | bytes 1966088 | tf_op jit(solution)/shard_map/ppermute | solution.py:273
  654.0 0.8 copy-start.2
  654.8 185.5 %collective-permute-start.4 = (bf16[4096,1024]{1,0:T(8,128)(2,1)}, bf16[4096,1024]{1,0:T(8,128)(2,1)}, u32[]{:S(2)}, u32[]{:S(2)}) collective-permute-start(bf16[4096,1024]{1,0:T(8,128)(2,1)} %slice.40), channel_id=1, source_target_pairs={{0,4},{1,5},{2,6},{3,7}} | collective-permute-start | bytes 25165832 | tf_op jit(solution)/shard_map/ppermute | solution.py:273
  666.9 19.0 %copy-start = (s32[312]{0:T(512)S(1)}, s32[312]{0:T(512)}, u32[]{:S(2)}) copy-start(s32[312]{0:T(512)} %constant.13.clone.tab) | copy-start | bytes 3748
  676.8 253.4 %collective-permute-start.3 = (bf16[4096,512]{1,0:T(8,128)(2,1)}, bf16[4096,512]{1,0:T(8,128)(2,1)}, u32[]{:S(2)}, u32[]{:S(2)}) collective-permute-start(bf16[4096,512]{1,0:T(8,128)(2,1)} %slice.41), channel_id=1, source_target_pairs={{0,4},{1,5},{2,6},{3,7}} | collective-permute-start | bytes 12582920 | tf_op jit(solution)/shard_map/ppermute | solution.py:273
  680.1 340.0 %collective-permute-start.9 = (bf16[4096,512]{1,0:T(8,128)(2,1)}, bf16[4096,512]{1,0:T(8,128)(2,1)}, u32[]{:S(2)}, u32[]{:S(2)}) collective-permute-start(bf16[4096,512]{1,0:T(8,128)(2,1)} %slice.42), channel_id=1, source_target_pairs={{0,4},{1,5},{2,6},{3,7}} | collective-permute-start | bytes 12582920 | tf_op jit(solution)/shard_map/ppermute | solution.py:273
  683.4 385.1 %collective-permute-start.10 = (bf16[2048,512]{1,0:T(8,128)(2,1)}, bf16[2048,512]{1,0:T(8,128)(2,1)}, u32[]{:S(2)}, u32[]{:S(2)}) collective-permute-start(bf16[2048,512]{1,0:T(8,128)(2,1)} %slice.43), channel_id=1, source_target_pairs={{0,4},{1,5},{2,6},{3,7}} | collective-permute-start | bytes 6291464 | tf_op jit(solution)/shard_map/ppermute | solution.py:273
  703.5 384.0 %collective-permute-start.11 = (bf16[1024,512]{1,0:T(8,128)(2,1)}, bf16[1024,512]{1,0:T(8,128)(2,1)}, u32[]{:S(2)}, u32[]{:S(2)}) collective-permute-start(bf16[1024,512]{1,0:T(8,128)(2,1)} %slice.44), channel_id=1, source_target_pairs={{0,4},{1,5},{2,6},{3,7}} | collective-permute-start | bytes 3145736 | tf_op jit(solution)/shard_map/ppermute | solution.py:273
  869.8 77.9 %copy-start.1 = (s32[120]{0:T(128)S(1)}, s32[120]{0:T(128)}, u32[]{:S(2)}) copy-start(s32[120]{0:T(128)} %constant.14.clone.tab) | copy-start | bytes 1444
  1038.7 60.0 %collective-permute-start.12 = (bf16[512,512]{1,0:T(8,128)(2,1)S(1)}, bf16[512,512]{1,0:T(8,128)(2,1)S(1)}, u32[]{:S(2)}, u32[]{:S(2)}) collective-permute-start(bf16[512,512]{1,0:T(8,128)(2,1)S(1)} %slice.45), channel_id=1, source_target_pairs={{0,4},{1,5},{2,6},{3,7}} | collective-permute-start | bytes 1572872 | tf_op jit(solution)/shard_map/ppermute | solution.py:273
  1065.8 43.9 %collective-permute-start.13 = (bf16[512,256]{1,0:T(8,128)(2,1)S(1)}, bf16[512,256]{1,0:T(8,128)(2,1)S(1)}, u32[]{:S(2)}, u32[]{:S(2)}) collective-permute-start(bf16[512,256]{1,0:T(8,128)(2,1)S(1)} %slice.47), channel_id=1, source_target_pairs={{0,4},{1,5},{2,6},{3,7}} | collective-permute-start | bytes 786440 | tf_op jit(solution)/shard_map/ppermute | solution.py:273
  1067.1 40.6 %collective-permute-start.14 = (bf16[512,256]{1,0:T(8,128)(2,1)S(1)}, bf16[512,256]{1,0:T(8,128)(2,1)S(1)}, u32[]{:S(2)}, u32[]{:S(2)}) collective-permute-start(bf16[512,256]{1,0:T(8,128)(2,1)S(1)} %slice.46), channel_id=1, source_target_pairs={{0,4},{1,5},{2,6},{3,7}} | collective-permute-start | bytes 786440 | tf_op jit(solution)/shard_map/ppermute | solution.py:273
where the time goes:
time: 1110 us
  waiting for transfers between devices  858 us (77%)
  Pallas kernels  138 us (12%)
  starting transfers between devices  77.3 us (7%)
  local copies, waits for them, and re-layouts  37.6 us (3%)
    ppermute x12, waiting for transfers between devices, send(): lax.ppermute(piece, 'row', [(0, 1), (1, 0)] if j == 0 else [(0, 1)])  498 us
    ppermute x1, waiting for transfers between devices, product(): lx = lax.ppermute(l_block, 'col', x_swap)  361 us
    pallas_call x6, Pallas kernels, chunk(): pl.pallas_call(functools.partial(chunk_kernel, half, depth, src0, dst0, w...  129 us
    ppermute x12, starting transfers between devices, send(): lax.ppermute(piece, 'row', [(0, 1), (1, 0)] if j == 0 else [(0, 1)])  74 us
    slice x12, local copies, waits for them, and re-layouts, send(): piece = source[r:r + h, c:c + w]  36.7 us
  transfers between devices with their start and end apart: 15, of which 9 were waited for; matrix products, arithmetic and copies ran while one was open for 3% of the time, Pallas kernels for 12%

commit v1 on v0

--- a/solution.py
+++ b/solution.py
@@ -161,8 +161,8 @@
             keep_copy(l0).wait()
 
 
-def tail_kernel(half, depth, k0, kw, src0, dst0, width, final, info, part, piece, *rest):
-    row, col = info[0], info[1]
+def tail_kernel(half, depth, k0, kw, src0, dst0, width, final, part, piece, *rest):
+    row, col = lax.axis_index('row'), lax.axis_index('col')
     tiles = half // TM
     kept = k0 >= half - KEEP
     if final:
@@ -311,9 +311,9 @@
 
         def tail(keep, piece, part, x, k0, kw, src0, width):
             final, kept = x is not None, k0 >= half - KEEP
-            operands = [info, part, pltpu.with_memory_space_constraint(piece, pltpu.VMEM) if kept else in_hbm(piece)]
+            operands = [part, pltpu.with_memory_space_constraint(piece, pltpu.VMEM) if kept else in_hbm(piece)]
             operands += [keep] if kept else list(map(in_hbm, l_refs))
-            specs = [smem, vmem] + ([vmem, vmem] if kept else [hbm] * 5)
+            specs = [vmem] + ([vmem, vmem] if kept else [hbm] * 5)
             scratch, need = [], 4 * TM * width + 2 * 2**20
             if final:
                 operands.append(x)
@@ -332,7 +332,7 @@
                 out_shape=out,
                 in_specs=specs, out_specs=out_spec,
                 scratch_shapes=scratch,
-                input_output_aliases={len(operands) - 1: 0} if final else {1: 0},
+                input_output_aliases={len(operands) - 1: 0} if final else {0: 0},
                 compiler_params=pltpu.CompilerParams(vmem_limit_bytes=need),
                 cost_estimate=pl.CostEstimate(flops=2 * half * kw * width,
                                               bytes_accessed=2 * half * kw, transcendentals=0),

time: 1110 us -> 1110 us (level)
  no operation moved by 1% of the time
where the time goes in v1:
time: 1110 us
  waiting for transfers between devices  860 us (77%)
  Pallas kernels  135 us (12%)
  starting transfers between devices  77.3 us (7%)
  local copies, waits for them, and re-layouts  37.6 us (3%)
    ppermute x12, waiting for transfers between devices, send(): lax.ppermute(piece, 'row', [(0, 1), (1, 0)] if j == 0 else [(0, 1)])  499 us
    ppermute x1, waiting for transfers between devices, product(): lx = lax.ppermute(l_block, 'col', x_swap)  361 us
    pallas_call x6, Pallas kernels, chunk(): pl.pallas_call(functools.partial(chunk_kernel, half, depth, src0, dst0, w...  129 us
    ppermute x12, starting transfers between devices, send(): lax.ppermute(piece, 'row', [(0, 1), (1, 0)] if j == 0 else [(0, 1)])  74 us
    slice x12, local copies, waits for them, and re-layouts, send(): piece = source[r:r + h, c:c + w]  36.7 us
  transfers between devices with their start and end apart: 15, of which 9 were waited for; matrix products, arithmetic and copies ran while one was open for 3% of the time, Pallas kernels for 12%

profile of v1, /device:TPU:0, one launch (start us, length us, event | category | flops | bytes accessed | tf_op | source)
XLA Modules:
  0.0 1110.7 jit_solution(12841642995187352761)
XLA Ops:
  0.0 3.3 collective-permute-start.1
  3.3 360.5 %collective-permute-done.1.l2.rest_2_ = bf16[4096,2048]{1,0:T(8,128)(2,1)} collective-permute-done((bf16[4096,2048]{1,0:T(8,128)(2,1)}, bf16[4096,2048]{1,0:T(8,128)(2,1)}, u32[]{:S(2)}, u32[]{:S(2)}) %collective-permute-start.1) | collective-permute-done | bytes 16777248 | tf_op jit(solution)/shard_map/ppermute | solution.py:279
  366.0 2.1 slice.38
  368.1 7.6 slice.39
  375.7 6.9 collective-permute-start.5
  382.6 2.9 collective-permute-start.8
  385.5 250.3 %collective-permute-done.6.rest_0_ = bf16[384,512]{1,0:T(8,128)(2,1)S(1)} collective-permute-done((bf16[384,512]{1,0:T(8,128)(2,1)S(1)}, bf16[384,512]{1,0:T(8,128)(2,1)S(1)}, u32[]{:S(2)}, u32[]{:S(2)}) %collective-permute-start.6) | collective-permute-done | bytes 393248 | tf_op jit(solution)/shard_map/ppermute | solution.py:273
  635.8 4.4 collective-permute-start.7
  640.2 7.6 slice.40
  647.8 6.1 collective-permute-done.7.rest_1_
  654.8 7.7 collective-permute-start.4
  662.5 4.4 slice.41
  666.9 4.5 slice.42
  671.4 3.1 slice.43
  674.4 2.3 slice.44
  676.8 3.3 collective-permute-start.3
  680.1 3.3 collective-permute-start.9
  683.4 2.6 collective-permute-start.10
  686.0 17.5 %shard_map.46.rest_1_ = bf16[4096,4096]{1,0:T(8,128)(2,1)} custom-call(s32[312]{0:T(512)S(1)} %copy-done, s32[2]{0:T(128)S(1)} %pad_add_fusion.info, bf16[4096,2048]{1,0:T(8,128)(2,1)} %rest_0_.3, bf16[4096,2048]{1,0:T(8,128)(2,1)} %collective-permute-done.l1.rest_1_, bf16[4096,2048]{1,0:T(8,128)(2,1)} %collective-permute-done.1.l2.rest_2_, ...), custom_call_target="tpu_custom_call" | custom-call | flops 27917287424 | bytes 54525952 | tf_op jit(solution)/shard_map/pallas_call | solution.py:301
  703.5 15.1 %collective-permute-start.11 = (bf16[1024,512]{1,0:T(8,128)(2,1)}, bf16[1024,512]{1,0:T(8,128)(2,1)}, u32[]{:S(2)}, u32[]{:S(2)}) collective-permute-start(bf16[1024,512]{1,0:T(8,128)(2,1)} %slice.44), channel_id=1, source_target_pairs={{0,4},{1,5},{2,6},{3,7}} | collective-permute-start | bytes 3145736 | tf_op jit(solution)/shard_map/ppermute | solution.py:273
  718.6 29.4 %shard_map.47.rest_1_ = bf16[4096,4096]{1,0:T(8,128)(2,1)} custom-call(s32[312]{0:T(512)S(1)} %copy-done, s32[2]{0:T(128)S(1)} %pad_add_fusion.info, bf16[4096,2048]{1,0:T(8,128)(2,1)} %rest_0_.3, bf16[4096,2048]{1,0:T(8,128)(2,1)} %collective-permute-done.l1.rest_1_, ...), custom_call_target="tpu_custom_call", output_to_operand_aliasing={{}: (8, {})} | custom-call | flops 55834574848 | bytes 54525952 | tf_op jit(solution)/shard_map/pallas_call | solution.py:301
  748.0 92.3 %collective-permute-done.4.rest_0_ = bf16[4096,1024]{1,0:T(8,128)(2,1)} collective-permute-done((bf16[4096,1024]{1,0:T(8,128)(2,1)}, bf16[4096,1024]{1,0:T(8,128)(2,1)}, u32[]{:S(2)}, u32[]{:S(2)}) %collective-permute-start.4) | collective-permute-done | bytes 8388640 | tf_op jit(solution)/shard_map/ppermute | solution.py:273
  840.3 29.4 %shard_map.48.rest_1_ = bf16[4096,4096]{1,0:T(8,128)(2,1)} custom-call(s32[312]{0:T(512)S(1)} %copy-done, s32[2]{0:T(128)S(1)} %pad_add_fusion.info, bf16[4096,2048]{1,0:T(8,128)(2,1)} %rest_0_.3, bf16[4096,2048]{1,0:T(8,128)(2,1)} %collective-permute-done.l1.rest_1_, ...), custom_call_target="tpu_custom_call", output_to_operand_aliasing={{}: (8, {})} | custom-call | flops 55834574848 | bytes 54525952 | tf_op jit(solution)/shard_map/pallas_call | solution.py:301
  869.8 60.4 %collective-permute-done.3.rest_0_ = bf16[4096,512]{1,0:T(8,128)(2,1)} collective-permute-done((bf16[4096,512]{1,0:T(8,128)(2,1)}, bf16[4096,512]{1,0:T(8,128)(2,1)}, u32[]{:S(2)}, u32[]{:S(2)}) %collective-permute-start.3) | collective-permute-done | bytes 4194336 | tf_op jit(solution)/shard_map/ppermute | solution.py:273
  930.2 17.5 %shard_map.49.rest_1_ = bf16[4096,4096]{1,0:T(8,128)(2,1)} custom-call(s32[312]{0:T(512)S(1)} %copy-done, s32[2]{0:T(128)S(1)} %pad_add_fusion.info, bf16[4096,2048]{1,0:T(8,128)(2,1)} %rest_0_.3, bf16[4096,2048]{1,0:T(8,128)(2,1)} %collective-permute-done.l1.rest_1_, ...), custom_call_target="tpu_custom_call", output_to_operand_aliasing={{}: (8, {})} | custom-call | flops 27917287424 | bytes 54525952 | tf_op jit(solution)/shard_map/pallas_call | solution.py:301
  947.7 17.8 %shard_map.50 = (f32[4096,512]{1,0:T(8,128)S(1)}, bf16[4096,1024]{1,0:T(8,128)(2,1)S(1)}) custom-call(s32[120]{0:T(128)S(1)} %copy-done.1, s32[2]{0:T(128)S(1)} %pad_add_fusion.info, bf16[4096,2048]{1,0:T(8,128)(2,1)} %rest_0_.3, bf16[4096,2048]{1,0:T(8,128)(2,1)} %collective-permute-done.l1.rest_1_, bf16[4096,2048]{1,0:T(8,128)(2,1)} %collective-permute-done.1.l2.rest_2_, ...), custom_call_target="tpu_custom_call" | custom-call | flops 10737418240 | bytes 20971520 | tf_op jit(solution)/shard_map/pallas_call | solution.py:301
  965.5 54.6 %collective-permute-done.9.rest_0_ = bf16[4096,512]{1,0:T(8,128)(2,1)} collective-permute-done((bf16[4096,512]{1,0:T(8,128)(2,1)}, bf16[4096,512]{1,0:T(8,128)(2,1)}, u32[]{:S(2)}, u32[]{:S(2)}) %collective-permute-start.9) | collective-permute-done | bytes 4194336 | tf_op jit(solution)/shard_map/ppermute | solution.py:273
  1020.1 17.5 %shard_map.51.rest_1_ = bf16[4096,4096]{1,0:T(8,128)(2,1)} custom-call(s32[312]{0:T(512)S(1)} %copy-done, s32[2]{0:T(128)S(1)} %pad_add_fusion.info, bf16[4096,2048]{1,0:T(8,128)(2,1)} %rest_0_.3, bf16[4096,2048]{1,0:T(8,128)(2,1)} %collective-permute-done.l1.rest_1_, ...), custom_call_target="tpu_custom_call", output_to_operand_aliasing={{}: (8, {})} | custom-call | flops 27917287424 | bytes 54525952 | tf_op jit(solution)/shard_map/pallas_call | solution.py:301
  1038.7 25.2 %collective-permute-start.12 = (bf16[512,512]{1,0:T(8,128)(2,1)S(1)}, bf16[512,512]{1,0:T(8,128)(2,1)S(1)}, u32[]{:S(2)}, u32[]{:S(2)}) collective-permute-start(bf16[512,512]{1,0:T(8,128)(2,1)S(1)} %slice.45), channel_id=1, source_target_pairs={{0,4},{1,5},{2,6},{3,7}} | collective-permute-start | bytes 1572872 | tf_op jit(solution)/shard_map/ppermute | solution.py:273
  1069.8 17.7 %collective-permute-done.11.piece = bf16[1024,512]{1,0:T(8,128)(2,1)} collective-permute-done((bf16[1024,512]{1,0:T(8,128)(2,1)}, bf16[1024,512]{1,0:T(8,128)(2,1)}, u32[]{:S(2)}, u32[]{:S(2)}) %collective-permute-start.11) | collective-permute-done | bytes 1048608 | tf_op jit(solution)/shard_map/ppermute | solution.py:273
  1088.6 10.0 collective-permute-done.12.piece
  1099.7 8.0 collective-permute-done.14.piece
  (30 shorter events, 15.1 us)
Async XLA Ops:
  0.0 363.8 %collective-permute-start.1 = (bf16[4096,2048]{1,0:T(8,128)(2,1)}, bf16[4096,2048]{1,0:T(8,128)(2,1)}, u32[]{:S(2)}, u32[]{:S(2)}) collective-permute-start(bf16[4096,2048]{1,0:T(8,128)(2,1)} %rest_0_.3), channel_id=1, source_target_pairs={{0,2},{1,3},{2,0},{3,1},{4,6},{5,7},{6,4},{7,5}} | collective-permute-start | bytes 50331656 | tf_op jit(solution)/shard_map/ppermute | solution.py:279
  3.3 676.8 %collective-permute-start = (bf16[4096,2048]{1,0:T(8,128)(2,1)}, bf16[4096,2048]{1,0:T(8,128)(2,1)}, u32[]{:S(2)}, u32[]{:S(2)}) collective-permute-start(bf16[4096,2048]{1,0:T(8,128)(2,1)} %rest_0_.3), channel_id=1, source_target_pairs={{0,1},{1,0},{2,3},{3,2},{4,5},{5,4},{6,7},{7,6}} | collective-permute-start | bytes 50331656 | tf_op jit(solution)/shard_map/ppermute | solution.py:280
  363.8 319.5 %collective-permute-start.2 = (bf16[4096,2048]{1,0:T(8,128)(2,1)}, bf16[4096,2048]{1,0:T(8,128)(2,1)}, u32[]{:S(2)}, u32[]{:S(2)}) collective-permute-start(bf16[4096,2048]{1,0:T(8,128)(2,1)} %collective-permute-done.1.l2.rest_2_), channel_id=1, source_target_pairs={{0,1},{1,0},{2,3},{3,2},{4,5},{5,4},{6,7},{7,6}} | collective-permute-start | bytes 50331656 | tf_op jit(solution)/shard_map/ppermute | solution.py:281
  375.7 327.8 %collective-permute-start.5 = (bf16[4096,1024]{1,0:T(8,128)(2,1)}, bf16[4096,1024]{1,0:T(8,128)(2,1)}, u32[]{:S(2)}, u32[]{:S(2)}) collective-permute-start(bf16[4096,1024]{1,0:T(8,128)(2,1)} %slice.39), channel_id=1, source_target_pairs={{0,4},{1,5},{2,6},{3,7}} | collective-permute-start | bytes 25165832 | tf_op jit(solution)/shard_map/ppermute | solution.py:273
  382.6 294.2 %collective-permute-start.8 = (bf16[3072,512]{1,0:T(8,128)(2,1)S(1)}, bf16[3072,512]{1,0:T(8,128)(2,1)}, u32[]{:S(2)}, u32[]{:S(2)}) collective-permute-start(bf16[3072,512]{1,0:T(8,128)(2,1)S(1)} %slice.38), channel_id=1, source_target_pairs={{0,4},{1,5},{2,6},{3,7}} | collective-permute-start | bytes 9437192 | tf_op jit(solution)/shard_map/ppermute | solution.py:273
  385.5 250.3 %collective-permute-start.6 = (bf16[384,512]{1,0:T(8,128)(2,1)S(1)}, bf16[384,512]{1,0:T(8,128)(2,1)S(1)}, u32[]{:S(2)}, u32[]{:S(2)}) collective-permute-start(bf16[384,512]{1,0:T(8,128)(2,1)S(1)} %slice.36), channel_id=1, source_target_pairs={{0,4},{4,0},{1,5},{5,1},{2,6},{6,2},{3,7},{7,3}} | collective-permute-start | bytes 1179656 | tf_op jit(solution)/shard_map/ppermute | solution.py:273
  635.8 12.0 %copy-start.3 = (bf16[384,512]{1,0:T(8,128)(2,1)}, bf16[384,512]{1,0:T(8,128)(2,1)S(1)}, u32[]{:S(2)}) copy-start(bf16[384,512]{1,0:T(8,128)(2,1)S(1)} %collective-permute-done.6.rest_0_) | copy-start | bytes 1179652
  635.8 18.2 %collective-permute-start.7 = (bf16[640,512]{1,0:T(8,128)(2,1)S(1)}, bf16[640,512]{1,0:T(8,128)(2,1)S(1)}, u32[]{:S(2)}, u32[]{:S(2)}) collective-permute-start(bf16[640,512]{1,0:T(8,128)(2,1)S(1)} %slice.37), channel_id=1, source_target_pairs={{0,4},{1,5},{2,6},{3,7}} | collective-permute-start | bytes 1966088 | tf_op jit(solution)/shard_map/ppermute | solution.py:273
  654.0 0.8 copy-start.2
  654.8 185.5 %collective-permute-start.4 = (bf16[4096,1024]{1,0:T(8,128)(2,1)}, bf16[4096,1024]{1,0:T(8,128)(2,1)}, u32[]{:S(2)}, u32[]{:S(2)}) collective-permute-start(bf16[4096,1024]{1,0:T(8,128)(2,1)} %slice.40), channel_id=1, source_target_pairs={{0,4},{1,5},{2,6},{3,7}} | collective-permute-start | bytes 25165832 | tf_op jit(solution)/shard_map/ppermute | solution.py:273
  666.9 19.0 %copy-start = (s32[312]{0:T(512)S(1)}, s32[312]{0:T(512)}, u32[]{:S(2)}) copy-start(s32[312]{0:T(512)} %constant.13.clone.tab) | copy-start | bytes 3748
  676.8 253.4 %collective-permute-start.3 = (bf16[4096,512]{1,0:T(8,128)(2,1)}, bf16[4096,512]{1,0:T(8,128)(2,1)}, u32[]{:S(2)}, u32[]{:S(2)}) collective-permute-start(bf16[4096,512]{1,0:T(8,128)(2,1)} %slice.41), channel_id=1, source_target_pairs={{0,4},{1,5},{2,6},{3,7}} | collective-permute-start | bytes 12582920 | tf_op jit(solution)/shard_map/ppermute | solution.py:273
  680.1 340.0 %collective-permute-start.9 = (bf16[4096,512]{1,0:T(8,128)(2,1)}, bf16[4096,512]{1,0:T(8,128)(2,1)}, u32[]{:S(2)}, u32[]{:S(2)}) collective-permute-start(bf16[4096,512]{1,0:T(8,128)(2,1)} %slice.42), channel_id=1, source_target_pairs={{0,4},{1,5},{2,6},{3,7}} | collective-permute-start | bytes 12582920 | tf_op jit(solution)/shard_map/ppermute | solution.py:273
  683.4 385.1 %collective-permute-start.10 = (bf16[2048,512]{1,0:T(8,128)(2,1)}, bf16[2048,512]{1,0:T(8,128)(2,1)}, u32[]{:S(2)}, u32[]{:S(2)}) collective-permute-start(bf16[2048,512]{1,0:T(8,128)(2,1)} %slice.43), channel_id=1, source_target_pairs={{0,4},{1,5},{2,6},{3,7}} | collective-permute-start | bytes 6291464 | tf_op jit(solution)/shard_map/ppermute | solution.py:273
  703.5 384.0 %collective-permute-start.11 = (bf16[1024,512]{1,0:T(8,128)(2,1)}, bf16[1024,512]{1,0:T(8,128)(2,1)}, u32[]{:S(2)}, u32[]{:S(2)}) collective-permute-start(bf16[1024,512]{1,0:T(8,128)(2,1)} %slice.44), channel_id=1, source_target_pairs={{0,4},{1,5},{2,6},{3,7}} | collective-permute-start | bytes 3145736 | tf_op jit(solution)/shard_map/ppermute | solution.py:273
  869.8 77.9 %copy-start.1 = (s32[120]{0:T(128)S(1)}, s32[120]{0:T(128)}, u32[]{:S(2)}) copy-start(s32[120]{0:T(128)} %constant.14.clone.tab) | copy-start | bytes 1444
  1038.7 60.0 %collective-permute-start.12 = (bf16[512,512]{1,0:T(8,128)(2,1)S(1)}, bf16[512,512]{1,0:T(8,128)(2,1)S(1)}, u32[]{:S(2)}, u32[]{:S(2)}) collective-permute-start(bf16[512,512]{1,0:T(8,128)(2,1)S(1)} %slice.45), channel_id=1, source_target_pairs={{0,4},{1,5},{2,6},{3,7}} | collective-permute-start | bytes 1572872 | tf_op jit(solution)/shard_map/ppermute | solution.py:273
  1065.8 43.3 %collective-permute-start.13 = (bf16[512,256]{1,0:T(8,128)(2,1)S(1)}, bf16[512,256]{1,0:T(8,128)(2,1)S(1)}, u32[]{:S(2)}, u32[]{:S(2)}) collective-permute-start(bf16[512,256]{1,0:T(8,128)(2,1)S(1)} %slice.47), channel_id=1, source_target_pairs={{0,4},{1,5},{2,6},{3,7}} | collective-permute-start | bytes 786440 | tf_op jit(solution)/shard_map/ppermute | solution.py:273
  1067.1 40.6 %collective-permute-start.14 = (bf16[512,256]{1,0:T(8,128)(2,1)S(1)}, bf16[512,256]{1,0:T(8,128)(2,1)S(1)}, u32[]{:S(2)}, u32[]{:S(2)}) collective-permute-start(bf16[512,256]{1,0:T(8,128)(2,1)S(1)} %slice.46), channel_id=1, source_target_pairs={{0,4},{1,5},{2,6},{3,7}} | collective-permute-start | bytes 786440 | tf_op jit(solution)/shard_map/ppermute | solution.py:273

commit v2 on v1

--- a/solution.py
+++ b/solution.py
@@ -16,7 +16,7 @@
 WIDTHS = (512, 1024, 1024, 512, 512)
 FIRST = (384, 640)
 TAIL = (2048, 1024, 512, 512)
-SPLIT = 2
+LAST = ((512,), (256, 256))
 KEEP = 1024
 DOT = functools.partial(jnp.dot, preferred_element_type=jnp.float32)
 
@@ -71,11 +71,15 @@
             b_loc.at[pl.ds(k * KB, KB), pl.ds(src0, width)], bv.at[pl.ds(slot * KB, KB), :], bsem.at[slot])
 
     def b_recv_start(k):
-        for ref, cut in zip(pieces, cuts):
-            lo, hi = max(k * KB, cut), min((k + 1) * KB, cut + ref.shape[0])
+        twins = len(cuts) > 1
+        ends = (cuts[2:3] + cuts[2:] if twins else ()) + (half,)
+        for i, (ref, cut, end) in enumerate(zip(pieces, cuts, ends)):
+            lo, hi = max(k * KB, cut), min((k + 1) * KB, end)
             if lo < hi:
-                pltpu.make_async_copy(
-                    ref.at[pl.ds(lo - cut, hi - lo), :], bv.at[pl.ds(lo, hi - lo), :], bsem.at[k]).start()
+                @pl.when(lax.rem(col, 2) == i if twins and i < 2 else True)
+                def _():
+                    pltpu.make_async_copy(
+                        ref.at[pl.ds(lo - cut, hi - lo), :], bv.at[pl.ds(lo, hi - lo), :], bsem.at[k]).start()
 
     def o_copy(r, slot):
         return pltpu.make_async_copy(
@@ -193,7 +197,7 @@
             ov[t] = total.astype(ov.dtype)
             o_copy(t).start()
         else:
-            out[rows, :] = total
+            out[rows, pl.ds(src0, width)] = total
 
     @pl.when(row == 1)
     def _():
@@ -262,19 +266,28 @@
         n_main = len(boxes)
         ends = np.cumsum(TAIL).tolist()
         boxes += [(e - h, h, tail0, tail_w) for e, h in zip(ends[:-1], TAIL)]
-        last_w = tail_w // SPLIT
-        boxes += [(half - TAIL[-1], TAIL[-1], tail0 + i * last_w, last_w) for i in range(SPLIT)]
+        last_w = tail_w // len(LAST)
+        n_early = len(boxes) - 1
+        for i, ks in enumerate(LAST):
+            boxes += [(half - TAIL[-1] + e - h, h, tail0 + i * last_w, last_w) for e, h in zip(np.cumsum(ks).tolist(), ks)]
         recv, source = [], b_block
 
         def send(j, source):
             r, h, c, w = boxes[j]
             piece = source[r:r + h, c:c + w]
             piece, source = lax.optimization_barrier((piece, source))
-            recv.append(lax.ppermute(piece, 'row', [(0, 1), (1, 0)] if j == 0 else [(0, 1)]))
+            recv.append(lax.ppermute(piece, 'row', [(0, 1)]))
             return source
 
-        n_early = len(boxes) - SPLIT - 1
-        for j in range(n_early):
+        first = []
+        for core in range(2):
+            piece = source[:FIRST[0], :WIDTHS[0]]
+            piece, source = lax.optimization_barrier((piece, source))
+            pairs = [(i, (i + 4) % 8 if i % 2 == core else i) for i in range(8)]
+            first.append(lax.ppermute(piece, ('row', 'col'), pairs))
+        recv.append(None)
+
+        for j in range(1, n_early):
             source = send(j, source)
         lx = lax.ppermute(l_block, 'col', x_swap)
         lc = lax.ppermute(l_block, 'col', core_swap)
@@ -347,13 +360,14 @@
                     source = send(i, source)
                 part, keep = chunk([], (), None, tail0, 0, tail_w, diag_counts, diag_tab)
                 x, part, keep = lax.optimization_barrier((x, part, keep))
-            pieces, cuts = (recv[:n_first], tuple(cuts0)) if j == 0 else ([recv[n_first - 1 + j]], (0,))
+            pieces, cuts = (first + recv[1:n_first], (0, 0) + tuple(cuts0[1:])) if j == 0 else ([recv[n_first - 1 + j]], (0,))
             x = chunk(pieces, cuts, x, starts[j], starts[j], width, off_counts, off_tab)
         x, part = lax.optimization_barrier((x, part))
-        for j, (piece, (k0, kw, c, w)) in enumerate(zip(recv[n_main:], boxes[n_main:])):
-            final = j >= len(TAIL) - 1
+        for piece, (k0, kw, c, w) in zip(recv[n_main:], boxes[n_main:]):
+            final = k0 + kw == half
             done = tail(keep, piece, part, x if final else None, k0, kw, c - tail0, w)
             part, x = (part, done) if final else (done, x)
+            x, part = lax.optimization_barrier((x, part))
         return x
 
     return jax.shard_map(product, mesh=mesh, in_specs=(block_spec, block_spec), out_specs=block_spec, check_vma=False)

time: 1110 us -> 1110 us (level)
  waiting for transfers between devices: 860 us -> 826 us
  starting transfers between devices: 77.3 us -> 108 us
    ppermute x12 -> x14, waiting for transfers between devices: 499 us -> 466 us  [the longest x2 248 us: product(): first.append(lax.ppermute(piece, ('row', 'col'), pairs))]
    ppermute x12 -> x14, starting transfers between devices: 74 us -> 104 us  [the longest x12 102 us: send(): recv.append(lax.ppermute(piece, 'row', [(0, 1)]))]
  transfers between devices with their start and end apart: 15 -> 17, of which waited for: 9 -> 9; matrix products, arithmetic and copies ran while one was open for 3% -> 3% of each run, Pallas kernels for 12% -> 12%
where the time goes in v2:
time: 1110 us
  waiting for transfers between devices  826 us (74%)
  Pallas kernels  136 us (12%)
  starting transfers between devices  108 us (10%)
  local copies, waits for them, and re-layouts  38.6 us (3%)
    ppermute x1, waiting for transfers between devices, product(): lx = lax.ppermute(l_block, 'col', x_swap)  361 us
    ppermute x2, waiting for transfers between devices, product(): first.append(lax.ppermute(piece, ('row', 'col'), pairs))  248 us
    ppermute x12, waiting for transfers between devices, send(): recv.append(lax.ppermute(piece, 'row', [(0, 1)]))  217 us
    pallas_call x6, Pallas kernels, chunk(): pl.pallas_call(functools.partial(chunk_kernel, half, depth, src0, dst0, w...  129 us
    ppermute x12, starting transfers between devices, send(): recv.append(lax.ppermute(piece, 'row', [(0, 1)]))  102 us
    slice x12, local copies, waits for them, and re-layouts, send(): piece = source[r:r + h, c:c + w]  36.5 us
  transfers between devices with their start and end apart: 17, of which 9 were waited for; matrix products, arithmetic and copies ran while one was open for 3% of the time, Pallas kernels for 12%

profile of v2, /device:TPU:0, one launch (start us, length us, event | category | flops | bytes accessed | tf_op | source)
XLA Modules:
  0.0 1108.9 jit_solution(18177455357306123420)
XLA Ops:
  0.0 3.3 collective-permute-start.1
  3.3 360.5 %collective-permute-done.1.l2.rest_2_ = bf16[4096,2048]{1,0:T(8,128)(2,1)} collective-permute-done((bf16[4096,2048]{1,0:T(8,128)(2,1)}, bf16[4096,2048]{1,0:T(8,128)(2,1)}, u32[]{:S(2)}, u32[]{:S(2)}) %collective-permute-start.1) | collective-permute-done | bytes 16777248 | tf_op jit(solution)/shard_map/ppermute | solution.py:292
  367.0 2.1 slice.45
  369.1 7.6 slice.46
  376.7 6.9 collective-permute-start.5
  383.6 2.9 collective-permute-start.9
  388.4 248.4 %collective-permute-done.6.rest_0_ = bf16[384,512]{1,0:T(8,128)(2,1)S(1)} collective-permute-done((bf16[384,512]{1,0:T(8,128)(2,1)S(1)}, bf16[384,512]{1,0:T(8,128)(2,1)S(1)}, u32[]{:S(2)}, u32[]{:S(2)}) %collective-permute-start.6) | collective-permute-done | bytes 393248 | tf_op jit(solution)/shard_map/ppermute | solution.py:287
  637.5 5.2 collective-permute-start.8
  642.7 7.6 slice.47
  650.4 4.6 collective-permute-done.8.rest_2_
  655.0 7.8 collective-permute-start.4
  662.8 4.4 slice.48
  667.2 4.5 slice.49
  671.6 3.0 slice.50
  674.7 2.3 slice.51
  677.1 3.3 collective-permute-start.3
  680.4 3.3 collective-permute-start.10
  683.6 2.6 collective-permute-start.11
  686.2 17.5 %shard_map.46.rest_1_ = bf16[4096,4096]{1,0:T(8,128)(2,1)} custom-call(s32[312]{0:T(512)S(1)} %copy-done, s32[2]{0:T(128)S(1)} %pad_add_fusion.info, bf16[4096,2048]{1,0:T(8,128)(2,1)} %rest_0_.3, bf16[4096,2048]{1,0:T(8,128)(2,1)} %collective-permute-done.l1.rest_1_, bf16[4096,2048]{1,0:T(8,128)(2,1)} %collective-permute-done.1.l2.rest_2_, ...), custom_call_target="tpu_custom_call" | custom-call | flops 27917287424 | bytes 54525952 | tf_op jit(solution)/shard_map/pallas_call | solution.py:314
  703.7 14.6 %collective-permute-start.12 = (bf16[1024,512]{1,0:T(8,128)(2,1)}, bf16[1024,512]{1,0:T(8,128)(2,1)}, u32[]{:S(2)}, u32[]{:S(2)}) collective-permute-start(bf16[1024,512]{1,0:T(8,128)(2,1)} %slice.51), channel_id=1, source_target_pairs={{0,4},{1,5},{2,6},{3,7}} | collective-permute-start | bytes 3145736 | tf_op jit(solution)/shard_map/ppermute | solution.py:279
  718.3 29.4 %shard_map.47.rest_1_ = bf16[4096,4096]{1,0:T(8,128)(2,1)} custom-call(s32[312]{0:T(512)S(1)} %copy-done, s32[2]{0:T(128)S(1)} %pad_add_fusion.info, bf16[4096,2048]{1,0:T(8,128)(2,1)} %rest_0_.3, bf16[4096,2048]{1,0:T(8,128)(2,1)} %collective-permute-done.l1.rest_1_, ...), custom_call_target="tpu_custom_call", output_to_operand_aliasing={{}: (8, {})} | custom-call | flops 55834574848 | bytes 54525952 | tf_op jit(solution)/shard_map/pallas_call | solution.py:314
  747.7 92.9 %collective-permute-done.4.rest_0_ = bf16[4096,1024]{1,0:T(8,128)(2,1)} collective-permute-done((bf16[4096,1024]{1,0:T(8,128)(2,1)}, bf16[4096,1024]{1,0:T(8,128)(2,1)}, u32[]{:S(2)}, u32[]{:S(2)}) %collective-permute-start.4) | collective-permute-done | bytes 8388640 | tf_op jit(solution)/shard_map/ppermute | solution.py:279
  840.6 29.4 %shard_map.48.rest_1_ = bf16[4096,4096]{1,0:T(8,128)(2,1)} custom-call(s32[312]{0:T(512)S(1)} %copy-done, s32[2]{0:T(128)S(1)} %pad_add_fusion.info, bf16[4096,2048]{1,0:T(8,128)(2,1)} %rest_0_.3, bf16[4096,2048]{1,0:T(8,128)(2,1)} %collective-permute-done.l1.rest_1_, ...), custom_call_target="tpu_custom_call", output_to_operand_aliasing={{}: (8, {})} | custom-call | flops 55834574848 | bytes 54525952 | tf_op jit(solution)/shard_map/pallas_call | solution.py:314
  870.1 60.4 %collective-permute-done.3.rest_0_ = bf16[4096,512]{1,0:T(8,128)(2,1)} collective-permute-done((bf16[4096,512]{1,0:T(8,128)(2,1)}, bf16[4096,512]{1,0:T(8,128)(2,1)}, u32[]{:S(2)}, u32[]{:S(2)}) %collective-permute-start.3) | collective-permute-done | bytes 4194336 | tf_op jit(solution)/shard_map/ppermute | solution.py:279
  930.5 17.5 %shard_map.49.rest_1_ = bf16[4096,4096]{1,0:T(8,128)(2,1)} custom-call(s32[312]{0:T(512)S(1)} %copy-done, s32[2]{0:T(128)S(1)} %pad_add_fusion.info, bf16[4096,2048]{1,0:T(8,128)(2,1)} %rest_0_.3, bf16[4096,2048]{1,0:T(8,128)(2,1)} %collective-permute-done.l1.rest_1_, ...), custom_call_target="tpu_custom_call", output_to_operand_aliasing={{}: (8, {})} | custom-call | flops 27917287424 | bytes 54525952 | tf_op jit(solution)/shard_map/pallas_call | solution.py:314
  948.0 17.8 %shard_map.50 = (f32[4096,512]{1,0:T(8,128)S(1)}, bf16[4096,1024]{1,0:T(8,128)(2,1)S(1)}) custom-call(s32[120]{0:T(128)S(1)} %copy-done.1, s32[2]{0:T(128)S(1)} %pad_add_fusion.info, bf16[4096,2048]{1,0:T(8,128)(2,1)} %rest_0_.3, bf16[4096,2048]{1,0:T(8,128)(2,1)} %collective-permute-done.l1.rest_1_, bf16[4096,2048]{1,0:T(8,128)(2,1)} %collective-permute-done.1.l2.rest_2_, ...), custom_call_target="tpu_custom_call" | custom-call | flops 10737418240 | bytes 20971520 | tf_op jit(solution)/shard_map/pallas_call | solution.py:314
  965.8 54.6 %collective-permute-done.10.rest_0_ = bf16[4096,512]{1,0:T(8,128)(2,1)} collective-permute-done((bf16[4096,512]{1,0:T(8,128)(2,1)}, bf16[4096,512]{1,0:T(8,128)(2,1)}, u32[]{:S(2)}, u32[]{:S(2)}) %collective-permute-start.10) | collective-permute-done | bytes 4194336 | tf_op jit(solution)/shard_map/ppermute | solution.py:279
  1020.4 17.5 %shard_map.51.rest_1_ = bf16[4096,4096]{1,0:T(8,128)(2,1)} custom-call(s32[312]{0:T(512)S(1)} %copy-done, s32[2]{0:T(128)S(1)} %pad_add_fusion.info, bf16[4096,2048]{1,0:T(8,128)(2,1)} %rest_0_.3, bf16[4096,2048]{1,0:T(8,128)(2,1)} %collective-permute-done.l1.rest_1_, ...), custom_call_target="tpu_custom_call", output_to_operand_aliasing={{}: (8, {})} | custom-call | flops 27917287424 | bytes 54525952 | tf_op jit(solution)/shard_map/pallas_call | solution.py:314
  1039.0 25.2 %collective-permute-start.13 = (bf16[512,512]{1,0:T(8,128)(2,1)S(1)}, bf16[512,512]{1,0:T(8,128)(2,1)S(1)}, u32[]{:S(2)}, u32[]{:S(2)}) collective-permute-start(bf16[512,512]{1,0:T(8,128)(2,1)S(1)} %slice.52), channel_id=1, source_target_pairs={{0,4},{1,5},{2,6},{3,7}} | collective-permute-start | bytes 1572872 | tf_op jit(solution)/shard_map/ppermute | solution.py:279
  1067.4 17.2 %collective-permute-start.14 = (bf16[512,256]{1,0:T(8,128)(2,1)S(1)}, bf16[512,256]{1,0:T(8,128)(2,1)S(1)}, u32[]{:S(2)}, u32[]{:S(2)}) collective-permute-start(bf16[512,256]{1,0:T(8,128)(2,1)S(1)} %slice.53), channel_id=1, source_target_pairs={{0,4},{1,5},{2,6},{3,7}} | collective-permute-start | bytes 786440 | tf_op jit(solution)/shard_map/ppermute | solution.py:279
  1084.6 3.2 collective-permute-done.12.piece
  1089.8 11.5 %collective-permute-start.15 = (bf16[256,256]{1,0:T(8,128)(2,1)S(1)}, bf16[256,256]{1,0:T(8,128)(2,1)S(1)}, u32[]{:S(2)}, u32[]{:S(2)}) collective-permute-start(bf16[256,256]{1,0:T(8,128)(2,1)S(1)} %slice.54), channel_id=1, source_target_pairs={{0,4},{1,5},{2,6},{3,7}} | collective-permute-start | bytes 393224 | tf_op jit(solution)/shard_map/ppermute | solution.py:279
  (37 shorter events, 19.6 us)
Async XLA Ops:
  0.0 363.8 %collective-permute-start.1 = (bf16[4096,2048]{1,0:T(8,128)(2,1)}, bf16[4096,2048]{1,0:T(8,128)(2,1)}, u32[]{:S(2)}, u32[]{:S(2)}) collective-permute-start(bf16[4096,2048]{1,0:T(8,128)(2,1)} %rest_0_.3), channel_id=1, source_target_pairs={{0,2},{1,3},{2,0},{3,1},{4,6},{5,7},{6,4},{7,5}} | collective-permute-start | bytes 50331656 | tf_op jit(solution)/shard_map/ppermute | solution.py:292
  3.3 677.1 %collective-permute-start = (bf16[4096,2048]{1,0:T(8,128)(2,1)}, bf16[4096,2048]{1,0:T(8,128)(2,1)}, u32[]{:S(2)}, u32[]{:S(2)}) collective-permute-start(bf16[4096,2048]{1,0:T(8,128)(2,1)} %rest_0_.3), channel_id=1, source_target_pairs={{0,1},{1,0},{2,3},{3,2},{4,5},{5,4},{6,7},{7,6}} | collective-permute-start | bytes 50331656 | tf_op jit(solution)/shard_map/ppermute | solution.py:293
  363.8 319.8 %collective-permute-start.2 = (bf16[4096,2048]{1,0:T(8,128)(2,1)}, bf16[4096,2048]{1,0:T(8,128)(2,1)}, u32[]{:S(2)}, u32[]{:S(2)}) collective-permute-start(bf16[4096,2048]{1,0:T(8,128)(2,1)} %collective-permute-done.1.l2.rest_2_), channel_id=1, source_target_pairs={{0,1},{1,0},{2,3},{3,2},{4,5},{5,4},{6,7},{7,6}} | collective-permute-start | bytes 50331656 | tf_op jit(solution)/shard_map/ppermute | solution.py:294
  376.7 327.0 %collective-permute-start.5 = (bf16[4096,1024]{1,0:T(8,128)(2,1)}, bf16[4096,1024]{1,0:T(8,128)(2,1)}, u32[]{:S(2)}, u32[]{:S(2)}) collective-permute-start(bf16[4096,1024]{1,0:T(8,128)(2,1)} %slice.46), channel_id=1, source_target_pairs={{0,4},{1,5},{2,6},{3,7}} | collective-permute-start | bytes 25165832 | tf_op jit(solution)/shard_map/ppermute | solution.py:279
  383.6 293.5 %collective-permute-start.9 = (bf16[3072,512]{1,0:T(8,128)(2,1)S(1)}, bf16[3072,512]{1,0:T(8,128)(2,1)}, u32[]{:S(2)}, u32[]{:S(2)}) collective-permute-start(bf16[3072,512]{1,0:T(8,128)(2,1)S(1)} %slice.45), channel_id=1, source_target_pairs={{0,4},{1,5},{2,6},{3,7}} | collective-permute-start | bytes 9437192 | tf_op jit(solution)/shard_map/ppermute | solution.py:279
  386.5 250.3 %collective-permute-start.6 = (bf16[384,512]{1,0:T(8,128)(2,1)S(1)}, bf16[384,512]{1,0:T(8,128)(2,1)S(1)}, u32[]{:S(2)}, u32[]{:S(2)}) collective-permute-start(bf16[384,512]{1,0:T(8,128)(2,1)S(1)} %slice.42), channel_id=1, source_target_pairs={{0,4},{1,1},{2,6},{3,3},{4,0},{5,5},{6,2},{7,7}} | collective-permute-start | bytes 1179656 | tf_op jit(solution)/shard_map/ppermute | solution.py:287
  636.8 13.5 %copy-start.2 = (bf16[384,512]{1,0:T(8,128)(2,1)}, bf16[384,512]{1,0:T(8,128)(2,1)S(1)}, u32[]{:S(2)}) copy-start(bf16[384,512]{1,0:T(8,128)(2,1)S(1)} %collective-permute-done.6.rest_0_) | copy-start | bytes 1179652
  636.8 0.7 collective-permute-start.7
  637.5 12.9 %copy-start.3 = (bf16[384,512]{1,0:T(8,128)(2,1)}, bf16[384,512]{1,0:T(8,128)(2,1)S(1)}, u32[]{:S(2)}) copy-start(bf16[384,512]{1,0:T(8,128)(2,1)S(1)} %collective-permute-done.7.rest_1_) | copy-start | bytes 1179652
  637.5 17.5 %collective-permute-start.8 = (bf16[640,512]{1,0:T(8,128)(2,1)S(1)}, bf16[640,512]{1,0:T(8,128)(2,1)}, u32[]{:S(2)}, u32[]{:S(2)}) collective-permute-start(bf16[640,512]{1,0:T(8,128)(2,1)S(1)} %slice.44), channel_id=1, source_target_pairs={{0,4},{1,5},{2,6},{3,7}} | collective-permute-start | bytes 1966088 | tf_op jit(solution)/shard_map/ppermute | solution.py:279
  655.0 185.6 %collective-permute-start.4 = (bf16[4096,1024]{1,0:T(8,128)(2,1)}, bf16[4096,1024]{1,0:T(8,128)(2,1)}, u32[]{:S(2)}, u32[]{:S(2)}) collective-permute-start(bf16[4096,1024]{1,0:T(8,128)(2,1)} %slice.47), channel_id=1, source_target_pairs={{0,4},{1,5},{2,6},{3,7}} | collective-permute-start | bytes 25165832 | tf_op jit(solution)/shard_map/ppermute | solution.py:279
  667.2 19.0 %copy-start = (s32[312]{0:T(512)S(1)}, s32[312]{0:T(512)}, u32[]{:S(2)}) copy-start(s32[312]{0:T(512)} %constant.13.clone.tab) | copy-start | bytes 3748
  677.1 253.4 %collective-permute-start.3 = (bf16[4096,512]{1,0:T(8,128)(2,1)}, bf16[4096,512]{1,0:T(8,128)(2,1)}, u32[]{:S(2)}, u32[]{:S(2)}) collective-permute-start(bf16[4096,512]{1,0:T(8,128)(2,1)} %slice.48), channel_id=1, source_target_pairs={{0,4},{1,5},{2,6},{3,7}} | collective-permute-start | bytes 12582920 | tf_op jit(solution)/shard_map/ppermute | solution.py:279
  680.4 340.0 %collective-permute-start.10 = (bf16[4096,512]{1,0:T(8,128)(2,1)}, bf16[4096,512]{1,0:T(8,128)(2,1)}, u32[]{:S(2)}, u32[]{:S(2)}) collective-permute-start(bf16[4096,512]{1,0:T(8,128)(2,1)} %slice.49), channel_id=1, source_target_pairs={{0,4},{1,5},{2,6},{3,7}} | collective-permute-start | bytes 12582920 | tf_op jit(solution)/shard_map/ppermute | solution.py:279
  683.6 381.7 %collective-permute-start.11 = (bf16[2048,512]{1,0:T(8,128)(2,1)}, bf16[2048,512]{1,0:T(8,128)(2,1)}, u32[]{:S(2)}, u32[]{:S(2)}) collective-permute-start(bf16[2048,512]{1,0:T(8,128)(2,1)} %slice.50), channel_id=1, source_target_pairs={{0,4},{1,5},{2,6},{3,7}} | collective-permute-start | bytes 6291464 | tf_op jit(solution)/shard_map/ppermute | solution.py:279
  703.7 384.1 %collective-permute-start.12 = (bf16[1024,512]{1,0:T(8,128)(2,1)}, bf16[1024,512]{1,0:T(8,128)(2,1)}, u32[]{:S(2)}, u32[]{:S(2)}) collective-permute-start(bf16[1024,512]{1,0:T(8,128)(2,1)} %slice.51), channel_id=1, source_target_pairs={{0,4},{1,5},{2,6},{3,7}} | collective-permute-start | bytes 3145736 | tf_op jit(solution)/shard_map/ppermute | solution.py:279
  870.1 77.9 %copy-start.1 = (s32[120]{0:T(128)S(1)}, s32[120]{0:T(128)}, u32[]{:S(2)}) copy-start(s32[120]{0:T(128)} %constant.14.clone.tab) | copy-start | bytes 1444
  1039.0 64.5 %collective-permute-start.13 = (bf16[512,512]{1,0:T(8,128)(2,1)S(1)}, bf16[512,512]{1,0:T(8,128)(2,1)S(1)}, u32[]{:S(2)}, u32[]{:S(2)}) collective-permute-start(bf16[512,512]{1,0:T(8,128)(2,1)S(1)} %slice.52), channel_id=1, source_target_pairs={{0,4},{1,5},{2,6},{3,7}} | collective-permute-start | bytes 1572872 | tf_op jit(solution)/shard_map/ppermute | solution.py:279
  1067.4 37.2 %collective-permute-start.14 = (bf16[512,256]{1,0:T(8,128)(2,1)S(1)}, bf16[512,256]{1,0:T(8,128)(2,1)S(1)}, u32[]{:S(2)}, u32[]{:S(2)}) collective-permute-start(bf16[512,256]{1,0:T(8,128)(2,1)S(1)} %slice.53), channel_id=1, source_target_pairs={{0,4},{1,5},{2,6},{3,7}} | collective-permute-start | bytes 786440 | tf_op jit(solution)/shard_map/ppermute | solution.py:279
  1089.8 16.2 %collective-permute-start.15 = (bf16[256,256]{1,0:T(8,128)(2,1)S(1)}, bf16[256,256]{1,0:T(8,128)(2,1)S(1)}, u32[]{:S(2)}, u32[]{:S(2)}) collective-permute-start(bf16[256,256]{1,0:T(8,128)(2,1)S(1)} %slice.54), channel_id=1, source_target_pairs={{0,4},{1,5},{2,6},{3,7}} | collective-permute-start | bytes 393224 | tf_op jit(solution)/shard_map/ppermute | solution.py:279
  1102.2 5.1 collective-permute-start.16

commit v3 on v1

--- a/solution.py
+++ b/solution.py
@@ -16,7 +16,7 @@
 WIDTHS = (512, 1024, 1024, 512, 512)
 FIRST = (384, 640)
 TAIL = (2048, 1024, 512, 512)
-SPLIT = 2
+LAST = ((256, (512,)), (256, (256, 256)))
 KEEP = 1024
 DOT = functools.partial(jnp.dot, preferred_element_type=jnp.float32)
 
@@ -193,7 +193,7 @@
             ov[t] = total.astype(ov.dtype)
             o_copy(t).start()
         else:
-            out[rows, :] = total
+            out[rows, pl.ds(src0, width)] = total
 
     @pl.when(row == 1)
     def _():
@@ -262,8 +262,10 @@
         n_main = len(boxes)
         ends = np.cumsum(TAIL).tolist()
         boxes += [(e - h, h, tail0, tail_w) for e, h in zip(ends[:-1], TAIL)]
-        last_w = tail_w // SPLIT
-        boxes += [(half - TAIL[-1], TAIL[-1], tail0 + i * last_w, last_w) for i in range(SPLIT)]
+        n_early, c = len(boxes) - 1, tail0
+        for w, ks in LAST:
+            boxes += [(half - TAIL[-1] + e - h, h, c, w) for e, h in zip(np.cumsum(ks).tolist(), ks)]
+            c += w
         recv, source = [], b_block
 
         def send(j, source):
@@ -273,7 +275,6 @@
             recv.append(lax.ppermute(piece, 'row', [(0, 1), (1, 0)] if j == 0 else [(0, 1)]))
             return source
 
-        n_early = len(boxes) - SPLIT - 1
         for j in range(n_early):
             source = send(j, source)
         lx = lax.ppermute(l_block, 'col', x_swap)
@@ -350,10 +351,11 @@
             pieces, cuts = (recv[:n_first], tuple(cuts0)) if j == 0 else ([recv[n_first - 1 + j]], (0,))
             x = chunk(pieces, cuts, x, starts[j], starts[j], width, off_counts, off_tab)
         x, part = lax.optimization_barrier((x, part))
-        for j, (piece, (k0, kw, c, w)) in enumerate(zip(recv[n_main:], boxes[n_main:])):
-            final = j >= len(TAIL) - 1
+        for piece, (k0, kw, c, w) in zip(recv[n_main:], boxes[n_main:]):
+            final = k0 + kw == half
             done = tail(keep, piece, part, x if final else None, k0, kw, c - tail0, w)
             part, x = (part, done) if final else (done, x)
+            x, part = lax.optimization_barrier((x, part))
         return x
 
     return jax.shard_map(product, mesh=mesh, in_specs=(block_spec, block_spec), out_specs=block_spec, check_vma=False)

time: 1110 us -> 1110 us (level)
  waiting for transfers between devices: 860 us -> 830 us
  starting transfers between devices: 77.3 us -> 105 us
    ppermute x12 -> x13, waiting for transfers between devices: 499 us -> 469 us  [send(): lax.ppermute(piece, 'row', [(0, 1), (1, 0)] if j == 0 else [(0, 1)])]
    ppermute x12 -> x13, starting transfers between devices: 74 us -> 101 us  [send(): lax.ppermute(piece, 'row', [(0, 1), (1, 0)] if j == 0 else [(0, 1)])]
    slice x12 -> x13, local copies, waits for them, and re-layouts: 36.7 us -> 37.6 us  [send(): piece = source[r:r + h, c:c + w]]
  transfers between devices with their start and end apart: 15 -> 16, of which waited for: 9 -> 10; matrix products, arithmetic and copies ran while one was open for 3% -> 3% of each run, Pallas kernels for 12% -> 12%
where the time goes in v3:
time: 1110 us
  waiting for transfers between devices  830 us (75%)
  Pallas kernels  136 us (12%)
  starting transfers between devices  105 us (9%)
  local copies, waits for them, and re-layouts  38.4 us (3%)
    ppermute x13, waiting for transfers between devices, send(): lax.ppermute(piece, 'row', [(0, 1), (1, 0)] if j == 0 else [(0, 1)])  469 us
    ppermute x1, waiting for transfers between devices, product(): lx = lax.ppermute(l_block, 'col', x_swap)  361 us
    pallas_call x6, Pallas kernels, chunk(): pl.pallas_call(functools.partial(chunk_kernel, half, depth, src0, dst0, w...  129 us
    ppermute x13, starting transfers between devices, send(): lax.ppermute(piece, 'row', [(0, 1), (1, 0)] if j == 0 else [(0, 1)])  101 us
    slice x13, local copies, waits for them, and re-layouts, send(): piece = source[r:r + h, c:c + w]  37.6 us
  transfers between devices with their start and end apart: 16, of which 10 were waited for; matrix products, arithmetic and copies ran while one was open for 3% of the time, Pallas kernels for 12%

profile of v3, /device:TPU:0, one launch (start us, length us, event | category | flops | bytes accessed | tf_op | source)
XLA Modules:
  0.0 1109.3 jit_solution(13744954214711354927)
XLA Ops:
  0.0 3.3 collective-permute-start.1
  3.3 360.5 %collective-permute-done.1.l2.rest_2_ = bf16[4096,2048]{1,0:T(8,128)(2,1)} collective-permute-done((bf16[4096,2048]{1,0:T(8,128)(2,1)}, bf16[4096,2048]{1,0:T(8,128)(2,1)}, u32[]{:S(2)}, u32[]{:S(2)}) %collective-permute-start.1) | collective-permute-done | bytes 16777248 | tf_op jit(solution)/shard_map/ppermute | solution.py:280
  366.0 2.1 slice.41
  368.1 7.6 slice.42
  375.7 6.9 collective-permute-start.5
  382.6 2.9 collective-permute-start.8
  385.5 250.3 %collective-permute-done.6.rest_0_ = bf16[384,512]{1,0:T(8,128)(2,1)S(1)} collective-permute-done((bf16[384,512]{1,0:T(8,128)(2,1)S(1)}, bf16[384,512]{1,0:T(8,128)(2,1)S(1)}, u32[]{:S(2)}, u32[]{:S(2)}) %collective-permute-start.6) | collective-permute-done | bytes 393248 | tf_op jit(solution)/shard_map/ppermute | solution.py:275
  635.8 4.4 collective-permute-start.7
  640.2 7.6 slice.43
  647.8 6.1 collective-permute-done.7.rest_1_
  654.8 7.7 collective-permute-start.4
  662.5 4.4 slice.44
  666.9 4.5 slice.45
  671.4 3.0 slice.46
  674.4 2.3 slice.47
  676.8 3.3 collective-permute-start.3
  680.1 3.3 collective-permute-start.9
  683.4 2.6 collective-permute-start.10
  686.0 17.5 %shard_map.46.rest_1_ = bf16[4096,4096]{1,0:T(8,128)(2,1)} custom-call(s32[312]{0:T(512)S(1)} %copy-done, s32[2]{0:T(128)S(1)} %pad_add_fusion.info, bf16[4096,2048]{1,0:T(8,128)(2,1)} %rest_0_.3, bf16[4096,2048]{1,0:T(8,128)(2,1)} %collective-permute-done.l1.rest_1_, bf16[4096,2048]{1,0:T(8,128)(2,1)} %collective-permute-done.1.l2.rest_2_, ...), custom_call_target="tpu_custom_call" | custom-call | flops 27917287424 | bytes 54525952 | tf_op jit(solution)/shard_map/pallas_call | solution.py:302
  703.5 15.1 %collective-permute-start.11 = (bf16[1024,512]{1,0:T(8,128)(2,1)}, bf16[1024,512]{1,0:T(8,128)(2,1)}, u32[]{:S(2)}, u32[]{:S(2)}) collective-permute-start(bf16[1024,512]{1,0:T(8,128)(2,1)} %slice.47), channel_id=1, source_target_pairs={{0,4},{1,5},{2,6},{3,7}} | collective-permute-start | bytes 3145736 | tf_op jit(solution)/shard_map/ppermute | solution.py:275
  718.6 29.4 %shard_map.47.rest_1_ = bf16[4096,4096]{1,0:T(8,128)(2,1)} custom-call(s32[312]{0:T(512)S(1)} %copy-done, s32[2]{0:T(128)S(1)} %pad_add_fusion.info, bf16[4096,2048]{1,0:T(8,128)(2,1)} %rest_0_.3, bf16[4096,2048]{1,0:T(8,128)(2,1)} %collective-permute-done.l1.rest_1_, ...), custom_call_target="tpu_custom_call", output_to_operand_aliasing={{}: (8, {})} | custom-call | flops 55834574848 | bytes 54525952 | tf_op jit(solution)/shard_map/pallas_call | solution.py:302
  748.0 92.3 %collective-permute-done.4.rest_0_ = bf16[4096,1024]{1,0:T(8,128)(2,1)} collective-permute-done((bf16[4096,1024]{1,0:T(8,128)(2,1)}, bf16[4096,1024]{1,0:T(8,128)(2,1)}, u32[]{:S(2)}, u32[]{:S(2)}) %collective-permute-start.4) | collective-permute-done | bytes 8388640 | tf_op jit(solution)/shard_map/ppermute | solution.py:275
  840.3 29.4 %shard_map.48.rest_1_ = bf16[4096,4096]{1,0:T(8,128)(2,1)} custom-call(s32[312]{0:T(512)S(1)} %copy-done, s32[2]{0:T(128)S(1)} %pad_add_fusion.info, bf16[4096,2048]{1,0:T(8,128)(2,1)} %rest_0_.3, bf16[4096,2048]{1,0:T(8,128)(2,1)} %collective-permute-done.l1.rest_1_, ...), custom_call_target="tpu_custom_call", output_to_operand_aliasing={{}: (8, {})} | custom-call | flops 55834574848 | bytes 54525952 | tf_op jit(solution)/shard_map/pallas_call | solution.py:302
  869.8 60.4 %collective-permute-done.3.rest_0_ = bf16[4096,512]{1,0:T(8,128)(2,1)} collective-permute-done((bf16[4096,512]{1,0:T(8,128)(2,1)}, bf16[4096,512]{1,0:T(8,128)(2,1)}, u32[]{:S(2)}, u32[]{:S(2)}) %collective-permute-start.3) | collective-permute-done | bytes 4194336 | tf_op jit(solution)/shard_map/ppermute | solution.py:275
  930.2 17.5 %shard_map.49.rest_1_ = bf16[4096,4096]{1,0:T(8,128)(2,1)} custom-call(s32[312]{0:T(512)S(1)} %copy-done, s32[2]{0:T(128)S(1)} %pad_add_fusion.info, bf16[4096,2048]{1,0:T(8,128)(2,1)} %rest_0_.3, bf16[4096,2048]{1,0:T(8,128)(2,1)} %collective-permute-done.l1.rest_1_, ...), custom_call_target="tpu_custom_call", output_to_operand_aliasing={{}: (8, {})} | custom-call | flops 27917287424 | bytes 54525952 | tf_op jit(solution)/shard_map/pallas_call | solution.py:302
  947.7 17.8 %shard_map.50 = (f32[4096,512]{1,0:T(8,128)S(1)}, bf16[4096,1024]{1,0:T(8,128)(2,1)S(1)}) custom-call(s32[120]{0:T(128)S(1)} %copy-done.1, s32[2]{0:T(128)S(1)} %pad_add_fusion.info, bf16[4096,2048]{1,0:T(8,128)(2,1)} %rest_0_.3, bf16[4096,2048]{1,0:T(8,128)(2,1)} %collective-permute-done.l1.rest_1_, bf16[4096,2048]{1,0:T(8,128)(2,1)} %collective-permute-done.1.l2.rest_2_, ...), custom_call_target="tpu_custom_call" | custom-call | flops 10737418240 | bytes 20971520 | tf_op jit(solution)/shard_map/pallas_call | solution.py:302
  965.5 54.6 %collective-permute-done.9.rest_0_ = bf16[4096,512]{1,0:T(8,128)(2,1)} collective-permute-done((bf16[4096,512]{1,0:T(8,128)(2,1)}, bf16[4096,512]{1,0:T(8,128)(2,1)}, u32[]{:S(2)}, u32[]{:S(2)}) %collective-permute-start.9) | collective-permute-done | bytes 4194336 | tf_op jit(solution)/shard_map/ppermute | solution.py:275
  1020.1 17.5 %shard_map.51.rest_1_ = bf16[4096,4096]{1,0:T(8,128)(2,1)} custom-call(s32[312]{0:T(512)S(1)} %copy-done, s32[2]{0:T(128)S(1)} %pad_add_fusion.info, bf16[4096,2048]{1,0:T(8,128)(2,1)} %rest_0_.3, bf16[4096,2048]{1,0:T(8,128)(2,1)} %collective-permute-done.l1.rest_1_, ...), custom_call_target="tpu_custom_call", output_to_operand_aliasing={{}: (8, {})} | custom-call | flops 27917287424 | bytes 54525952 | tf_op jit(solution)/shard_map/pallas_call | solution.py:302
  1038.7 25.2 %collective-permute-start.12 = (bf16[512,512]{1,0:T(8,128)(2,1)S(1)}, bf16[512,512]{1,0:T(8,128)(2,1)S(1)}, u32[]{:S(2)}, u32[]{:S(2)}) collective-permute-start(bf16[512,512]{1,0:T(8,128)(2,1)S(1)} %slice.48), channel_id=1, source_target_pairs={{0,4},{1,5},{2,6},{3,7}} | collective-permute-start | bytes 1572872 | tf_op jit(solution)/shard_map/ppermute | solution.py:275
  1067.1 17.2 %collective-permute-start.13 = (bf16[512,256]{1,0:T(8,128)(2,1)S(1)}, bf16[512,256]{1,0:T(8,128)(2,1)S(1)}, u32[]{:S(2)}, u32[]{:S(2)}) collective-permute-start(bf16[512,256]{1,0:T(8,128)(2,1)S(1)} %slice.49), channel_id=1, source_target_pairs={{0,4},{1,5},{2,6},{3,7}} | collective-permute-start | bytes 786440 | tf_op jit(solution)/shard_map/ppermute | solution.py:275
  1084.4 3.2 collective-permute-done.11.piece
  1089.5 11.5 %collective-permute-start.14 = (bf16[256,256]{1,0:T(8,128)(2,1)S(1)}, bf16[256,256]{1,0:T(8,128)(2,1)S(1)}, u32[]{:S(2)}, u32[]{:S(2)}) collective-permute-start(bf16[256,256]{1,0:T(8,128)(2,1)S(1)} %slice.50), channel_id=1, source_target_pairs={{0,4},{1,5},{2,6},{3,7}} | collective-permute-start | bytes 393224 | tf_op jit(solution)/shard_map/ppermute | solution.py:275
  (34 shorter events, 17.5 us)
Async XLA Ops:
  0.0 363.8 %collective-permute-start.1 = (bf16[4096,2048]{1,0:T(8,128)(2,1)}, bf16[4096,2048]{1,0:T(8,128)(2,1)}, u32[]{:S(2)}, u32[]{:S(2)}) collective-permute-start(bf16[4096,2048]{1,0:T(8,128)(2,1)} %rest_0_.3), channel_id=1, source_target_pairs={{0,2},{1,3},{2,0},{3,1},{4,6},{5,7},{6,4},{7,5}} | collective-permute-start | bytes 50331656 | tf_op jit(solution)/shard_map/ppermute | solution.py:280
  3.3 676.8 %collective-permute-start = (bf16[4096,2048]{1,0:T(8,128)(2,1)}, bf16[4096,2048]{1,0:T(8,128)(2,1)}, u32[]{:S(2)}, u32[]{:S(2)}) collective-permute-start(bf16[4096,2048]{1,0:T(8,128)(2,1)} %rest_0_.3), channel_id=1, source_target_pairs={{0,1},{1,0},{2,3},{3,2},{4,5},{5,4},{6,7},{7,6}} | collective-permute-start | bytes 50331656 | tf_op jit(solution)/shard_map/ppermute | solution.py:281
  363.8 319.5 %collective-permute-start.2 = (bf16[4096,2048]{1,0:T(8,128)(2,1)}, bf16[4096,2048]{1,0:T(8,128)(2,1)}, u32[]{:S(2)}, u32[]{:S(2)}) collective-permute-start(bf16[4096,2048]{1,0:T(8,128)(2,1)} %collective-permute-done.1.l2.rest_2_), channel_id=1, source_target_pairs={{0,1},{1,0},{2,3},{3,2},{4,5},{5,4},{6,7},{7,6}} | collective-permute-start | bytes 50331656 | tf_op jit(solution)/shard_map/ppermute | solution.py:282
  375.7 327.8 %collective-permute-start.5 = (bf16[4096,1024]{1,0:T(8,128)(2,1)}, bf16[4096,1024]{1,0:T(8,128)(2,1)}, u32[]{:S(2)}, u32[]{:S(2)}) collective-permute-start(bf16[4096,1024]{1,0:T(8,128)(2,1)} %slice.42), channel_id=1, source_target_pairs={{0,4},{1,5},{2,6},{3,7}} | collective-permute-start | bytes 25165832 | tf_op jit(solution)/shard_map/ppermute | solution.py:275
  382.6 294.2 %collective-permute-start.8 = (bf16[3072,512]{1,0:T(8,128)(2,1)S(1)}, bf16[3072,512]{1,0:T(8,128)(2,1)}, u32[]{:S(2)}, u32[]{:S(2)}) collective-permute-start(bf16[3072,512]{1,0:T(8,128)(2,1)S(1)} %slice.41), channel_id=1, source_target_pairs={{0,4},{1,5},{2,6},{3,7}} | collective-permute-start | bytes 9437192 | tf_op jit(solution)/shard_map/ppermute | solution.py:275
  385.5 250.3 %collective-permute-start.6 = (bf16[384,512]{1,0:T(8,128)(2,1)S(1)}, bf16[384,512]{1,0:T(8,128)(2,1)S(1)}, u32[]{:S(2)}, u32[]{:S(2)}) collective-permute-start(bf16[384,512]{1,0:T(8,128)(2,1)S(1)} %slice.39), channel_id=1, source_target_pairs={{0,4},{4,0},{1,5},{5,1},{2,6},{6,2},{3,7},{7,3}} | collective-permute-start | bytes 1179656 | tf_op jit(solution)/shard_map/ppermute | solution.py:275
  635.8 12.0 %copy-start.3 = (bf16[384,512]{1,0:T(8,128)(2,1)}, bf16[384,512]{1,0:T(8,128)(2,1)S(1)}, u32[]{:S(2)}) copy-start(bf16[384,512]{1,0:T(8,128)(2,1)S(1)} %collective-permute-done.6.rest_0_) | copy-start | bytes 1179652
  635.8 18.2 %collective-permute-start.7 = (bf16[640,512]{1,0:T(8,128)(2,1)S(1)}, bf16[640,512]{1,0:T(8,128)(2,1)S(1)}, u32[]{:S(2)}, u32[]{:S(2)}) collective-permute-start(bf16[640,512]{1,0:T(8,128)(2,1)S(1)} %slice.40), channel_id=1, source_target_pairs={{0,4},{1,5},{2,6},{3,7}} | collective-permute-start | bytes 1966088 | tf_op jit(solution)/shard_map/ppermute | solution.py:275
  654.0 0.8 copy-start.2
  654.8 185.5 %collective-permute-start.4 = (bf16[4096,1024]{1,0:T(8,128)(2,1)}, bf16[4096,1024]{1,0:T(8,128)(2,1)}, u32[]{:S(2)}, u32[]{:S(2)}) collective-permute-start(bf16[4096,1024]{1,0:T(8,128)(2,1)} %slice.43), channel_id=1, source_target_pairs={{0,4},{1,5},{2,6},{3,7}} | collective-permute-start | bytes 25165832 | tf_op jit(solution)/shard_map/ppermute | solution.py:275
  666.9 19.0 %copy-start = (s32[312]{0:T(512)S(1)}, s32[312]{0:T(512)}, u32[]{:S(2)}) copy-start(s32[312]{0:T(512)} %constant.13.clone.tab) | copy-start | bytes 3748
  676.8 253.4 %collective-permute-start.3 = (bf16[4096,512]{1,0:T(8,128)(2,1)}, bf16[4096,512]{1,0:T(8,128)(2,1)}, u32[]{:S(2)}, u32[]{:S(2)}) collective-permute-start(bf16[4096,512]{1,0:T(8,128)(2,1)} %slice.44), channel_id=1, source_target_pairs={{0,4},{1,5},{2,6},{3,7}} | collective-permute-start | bytes 12582920 | tf_op jit(solution)/shard_map/ppermute | solution.py:275
  680.1 340.0 %collective-permute-start.9 = (bf16[4096,512]{1,0:T(8,128)(2,1)}, bf16[4096,512]{1,0:T(8,128)(2,1)}, u32[]{:S(2)}, u32[]{:S(2)}) collective-permute-start(bf16[4096,512]{1,0:T(8,128)(2,1)} %slice.45), channel_id=1, source_target_pairs={{0,4},{1,5},{2,6},{3,7}} | collective-permute-start | bytes 12582920 | tf_op jit(solution)/shard_map/ppermute | solution.py:275
  683.4 381.7 %collective-permute-start.10 = (bf16[2048,512]{1,0:T(8,128)(2,1)}, bf16[2048,512]{1,0:T(8,128)(2,1)}, u32[]{:S(2)}, u32[]{:S(2)}) collective-permute-start(bf16[2048,512]{1,0:T(8,128)(2,1)} %slice.46), channel_id=1, source_target_pairs={{0,4},{1,5},{2,6},{3,7}} | collective-permute-start | bytes 6291464 | tf_op jit(solution)/shard_map/ppermute | solution.py:275
  703.5 384.0 %collective-permute-start.11 = (bf16[1024,512]{1,0:T(8,128)(2,1)}, bf16[1024,512]{1,0:T(8,128)(2,1)}, u32[]{:S(2)}, u32[]{:S(2)}) collective-permute-start(bf16[1024,512]{1,0:T(8,128)(2,1)} %slice.47), channel_id=1, source_target_pairs={{0,4},{1,5},{2,6},{3,7}} | collective-permute-start | bytes 3145736 | tf_op jit(solution)/shard_map/ppermute | solution.py:275
  869.8 77.9 %copy-start.1 = (s32[120]{0:T(128)S(1)}, s32[120]{0:T(128)}, u32[]{:S(2)}) copy-start(s32[120]{0:T(128)} %constant.14.clone.tab) | copy-start | bytes 1444
  1038.7 64.5 %collective-permute-start.12 = (bf16[512,512]{1,0:T(8,128)(2,1)S(1)}, bf16[512,512]{1,0:T(8,128)(2,1)S(1)}, u32[]{:S(2)}, u32[]{:S(2)}) collective-permute-start(bf16[512,512]{1,0:T(8,128)(2,1)S(1)} %slice.48), channel_id=1, source_target_pairs={{0,4},{1,5},{2,6},{3,7}} | collective-permute-start | bytes 1572872 | tf_op jit(solution)/shard_map/ppermute | solution.py:275
  1067.1 37.2 %collective-permute-start.13 = (bf16[512,256]{1,0:T(8,128)(2,1)S(1)}, bf16[512,256]{1,0:T(8,128)(2,1)S(1)}, u32[]{:S(2)}, u32[]{:S(2)}) collective-permute-start(bf16[512,256]{1,0:T(8,128)(2,1)S(1)} %slice.49), channel_id=1, source_target_pairs={{0,4},{1,5},{2,6},{3,7}} | collective-permute-start | bytes 786440 | tf_op jit(solution)/shard_map/ppermute | solution.py:275
  1089.5 16.8 %collective-permute-start.14 = (bf16[256,256]{1,0:T(8,128)(2,1)S(1)}, bf16[256,256]{1,0:T(8,128)(2,1)S(1)}, u32[]{:S(2)}, u32[]{:S(2)}) collective-permute-start(bf16[256,256]{1,0:T(8,128)(2,1)S(1)} %slice.50), channel_id=1, source_target_pairs={{0,4},{1,5},{2,6},{3,7}} | collective-permute-start | bytes 393224 | tf_op jit(solution)/shard_map/ppermute | solution.py:275
  1101.9 5.8 collective-permute-start.15

commit v4 on v3

--- a/solution.py
+++ b/solution.py
@@ -161,7 +161,7 @@
             keep_copy(l0).wait()
 
 
-def tail_kernel(half, depth, k0, kw, src0, dst0, width, final, part, piece, *rest):
+def tail_kernel(half, depth, k0, kw, src0, dst0, width, final, early, part, piece, *rest):
     row, col = lax.axis_index('row'), lax.axis_index('col')
     tiles = half // TM
     kept = k0 >= half - KEEP
@@ -184,9 +184,9 @@
             def _():
                 l_copy(ref, t).start()
 
-    def o_copy(t):
+    def o_copy(t, c=src0):
         return pltpu.make_async_copy(
-            ov.at[t], out.at[pl.ds(t * TM, TM), pl.ds(dst0, width)], osem.at[t])
+            ov.at[t], out.at[pl.ds(t * TM, TM), pl.ds(dst0 + c, width)], osem.at[t])
 
     def put(t, rows, total):
         if final:
@@ -221,18 +221,25 @@
 
         lax.fori_loop(0, tiles, add, 0, unroll=kept)
 
-    @pl.when(row == 0)
-    def _():
-        def move(t, _):
-            rows = pl.ds(pl.multiple_of(t * TM, TM), TM)
-            put(t, rows, part[rows, pl.ds(src0, width)])
-            return 0
-
-        lax.fori_loop(0, tiles, move, 0)
-
     if final:
-        for t in range(tiles):
-            o_copy(t).wait()
+        @pl.when(row == 1)
+        def _():
+            for t in range(tiles):
+                o_copy(t).wait()
+
+    if early:
+        @pl.when(row == 0)
+        def _():
+            for c in range(0, part.shape[1], width):
+                def move(t, _):
+                    rows = pl.ds(pl.multiple_of(t * TM, TM), TM)
+                    ov[t] = part[rows, pl.ds(c, width)].astype(ov.dtype)
+                    o_copy(t, c).start()
+                    return 0
+
+                lax.fori_loop(0, tiles, move, 0)
+                for t in range(tiles):
+                    o_copy(t, c).wait()
 
 
 def solution(mesh):
@@ -329,7 +336,7 @@
                                pltpu.SemaphoreType.DMA((2,)), pltpu.SemaphoreType.DMA]
                     need += 2 * kw * (width + 2 * TM)
             return pl.pallas_call(
-                functools.partial(tail_kernel, half, depth, k0, kw, src0, tail0 + src0, width, final),
+                functools.partial(tail_kernel, half, depth, k0, kw, src0, tail0, width, final, final and src0 == 0),
                 out_shape=out,
                 in_specs=specs, out_specs=out_spec,
                 scratch_shapes=scratch,

time: 1110 us -> 1110 us (level)
  no operation moved by 1% of the time
where the time goes in v4:
time: 1110 us
  waiting for transfers between devices  830 us (75%)
  Pallas kernels  132 us (12%)
  starting transfers between devices  107 us (10%)
  local copies, waits for them, and re-layouts  38.4 us (3%)
    ppermute x13, waiting for transfers between devices, send(): lax.ppermute(piece, 'row', [(0, 1), (1, 0)] if j == 0 else [(0, 1)])  470 us
    ppermute x1, waiting for transfers between devices, product(): lx = lax.ppermute(l_block, 'col', x_swap)  361 us
    pallas_call x6, Pallas kernels, chunk(): pl.pallas_call(functools.partial(chunk_kernel, half, depth, src0, dst0, w...  129 us
    ppermute x13, starting transfers between devices, send(): lax.ppermute(piece, 'row', [(0, 1), (1, 0)] if j == 0 else [(0, 1)])  103 us
    slice x13, local copies, waits for them, and re-layouts, send(): piece = source[r:r + h, c:c + w]  37.6 us
  transfers between devices with their start and end apart: 16, of which 10 were waited for; matrix products, arithmetic and copies ran while one was open for 3% of the time, Pallas kernels for 12%

profile of v4, /device:TPU:0, one launch (start us, length us, event | category | flops | bytes accessed | tf_op | source)
XLA Modules:
  0.0 1107.9 jit_solution(6954034426727008059)
XLA Ops:
  0.0 3.3 collective-permute-start.1
  3.3 360.5 %collective-permute-done.1.l2.rest_2_ = bf16[4096,2048]{1,0:T(8,128)(2,1)} collective-permute-done((bf16[4096,2048]{1,0:T(8,128)(2,1)}, bf16[4096,2048]{1,0:T(8,128)(2,1)}, u32[]{:S(2)}, u32[]{:S(2)}) %collective-permute-start.1) | collective-permute-done | bytes 16777248 | tf_op jit(solution)/shard_map/ppermute | solution.py:287
  368.1 7.6 slice.42
  375.7 6.9 collective-permute-start.5
  382.6 2.9 collective-permute-start.8
  385.5 250.3 %collective-permute-done.6.rest_0_ = bf16[384,512]{1,0:T(8,128)(2,1)S(1)} collective-permute-done((bf16[384,512]{1,0:T(8,128)(2,1)S(1)}, bf16[384,512]{1,0:T(8,128)(2,1)S(1)}, u32[]{:S(2)}, u32[]{:S(2)}) %collective-permute-start.6) | collective-permute-done | bytes 393248 | tf_op jit(solution)/shard_map/ppermute | solution.py:282
  635.8 4.4 collective-permute-start.7
  640.2 7.6 slice.43
  647.8 6.1 collective-permute-done.7.rest_1_
  654.8 7.7 collective-permute-start.4
  662.5 4.4 slice.44
  666.9 4.5 slice.45
  671.4 3.0 slice.46
  674.4 2.3 slice.47
  676.8 3.3 collective-permute-start.3
  680.1 3.3 collective-permute-start.9
  683.4 2.6 collective-permute-start.10
  686.0 17.5 %shard_map.46.rest_1_ = bf16[4096,4096]{1,0:T(8,128)(2,1)} custom-call(s32[312]{0:T(512)S(1)} %copy-done, s32[2]{0:T(128)S(1)} %pad_add_fusion.info, bf16[4096,2048]{1,0:T(8,128)(2,1)} %rest_0_.3, bf16[4096,2048]{1,0:T(8,128)(2,1)} %collective-permute-done.l1.rest_1_, bf16[4096,2048]{1,0:T(8,128)(2,1)} %collective-permute-done.1.l2.rest_2_, ...), custom_call_target="tpu_custom_call" | custom-call | flops 27917287424 | bytes 54525952 | tf_op jit(solution)/shard_map/pallas_call | solution.py:309
  703.5 15.1 %collective-permute-start.11 = (bf16[1024,512]{1,0:T(8,128)(2,1)}, bf16[1024,512]{1,0:T(8,128)(2,1)}, u32[]{:S(2)}, u32[]{:S(2)}) collective-permute-start(bf16[1024,512]{1,0:T(8,128)(2,1)} %slice.47), channel_id=1, source_target_pairs={{0,4},{1,5},{2,6},{3,7}} | collective-permute-start | bytes 3145736 | tf_op jit(solution)/shard_map/ppermute | solution.py:282
  718.6 29.4 %shard_map.47.rest_1_ = bf16[4096,4096]{1,0:T(8,128)(2,1)} custom-call(s32[312]{0:T(512)S(1)} %copy-done, s32[2]{0:T(128)S(1)} %pad_add_fusion.info, bf16[4096,2048]{1,0:T(8,128)(2,1)} %rest_0_.3, bf16[4096,2048]{1,0:T(8,128)(2,1)} %collective-permute-done.l1.rest_1_, ...), custom_call_target="tpu_custom_call", output_to_operand_aliasing={{}: (8, {})} | custom-call | flops 55834574848 | bytes 54525952 | tf_op jit(solution)/shard_map/pallas_call | solution.py:309
  748.0 92.3 %collective-permute-done.4.rest_0_ = bf16[4096,1024]{1,0:T(8,128)(2,1)} collective-permute-done((bf16[4096,1024]{1,0:T(8,128)(2,1)}, bf16[4096,1024]{1,0:T(8,128)(2,1)}, u32[]{:S(2)}, u32[]{:S(2)}) %collective-permute-start.4) | collective-permute-done | bytes 8388640 | tf_op jit(solution)/shard_map/ppermute | solution.py:282
  840.3 29.4 %shard_map.48.rest_1_ = bf16[4096,4096]{1,0:T(8,128)(2,1)} custom-call(s32[312]{0:T(512)S(1)} %copy-done, s32[2]{0:T(128)S(1)} %pad_add_fusion.info, bf16[4096,2048]{1,0:T(8,128)(2,1)} %rest_0_.3, bf16[4096,2048]{1,0:T(8,128)(2,1)} %collective-permute-done.l1.rest_1_, ...), custom_call_target="tpu_custom_call", output_to_operand_aliasing={{}: (8, {})} | custom-call | flops 55834574848 | bytes 54525952 | tf_op jit(solution)/shard_map/pallas_call | solution.py:309
  869.8 60.4 %collective-permute-done.3.rest_0_ = bf16[4096,512]{1,0:T(8,128)(2,1)} collective-permute-done((bf16[4096,512]{1,0:T(8,128)(2,1)}, bf16[4096,512]{1,0:T(8,128)(2,1)}, u32[]{:S(2)}, u32[]{:S(2)}) %collective-permute-start.3) | collective-permute-done | bytes 4194336 | tf_op jit(solution)/shard_map/ppermute | solution.py:282
  930.2 17.5 %shard_map.49.rest_1_ = bf16[4096,4096]{1,0:T(8,128)(2,1)} custom-call(s32[312]{0:T(512)S(1)} %copy-done, s32[2]{0:T(128)S(1)} %pad_add_fusion.info, bf16[4096,2048]{1,0:T(8,128)(2,1)} %rest_0_.3, bf16[4096,2048]{1,0:T(8,128)(2,1)} %collective-permute-done.l1.rest_1_, ...), custom_call_target="tpu_custom_call", output_to_operand_aliasing={{}: (8, {})} | custom-call | flops 27917287424 | bytes 54525952 | tf_op jit(solution)/shard_map/pallas_call | solution.py:309
  947.7 17.8 %shard_map.50 = (f32[4096,512]{1,0:T(8,128)S(1)}, bf16[4096,1024]{1,0:T(8,128)(2,1)S(1)}) custom-call(s32[120]{0:T(128)S(1)} %copy-done.1, s32[2]{0:T(128)S(1)} %pad_add_fusion.info, bf16[4096,2048]{1,0:T(8,128)(2,1)} %rest_0_.3, bf16[4096,2048]{1,0:T(8,128)(2,1)} %collective-permute-done.l1.rest_1_, bf16[4096,2048]{1,0:T(8,128)(2,1)} %collective-permute-done.1.l2.rest_2_, ...), custom_call_target="tpu_custom_call" | custom-call | flops 10737418240 | bytes 20971520 | tf_op jit(solution)/shard_map/pallas_call | solution.py:309
  965.5 54.6 %collective-permute-done.9.rest_0_ = bf16[4096,512]{1,0:T(8,128)(2,1)} collective-permute-done((bf16[4096,512]{1,0:T(8,128)(2,1)}, bf16[4096,512]{1,0:T(8,128)(2,1)}, u32[]{:S(2)}, u32[]{:S(2)}) %collective-permute-start.9) | collective-permute-done | bytes 4194336 | tf_op jit(solution)/shard_map/ppermute | solution.py:282
  1020.1 17.5 %shard_map.51.rest_1_ = bf16[4096,4096]{1,0:T(8,128)(2,1)} custom-call(s32[312]{0:T(512)S(1)} %copy-done, s32[2]{0:T(128)S(1)} %pad_add_fusion.info, bf16[4096,2048]{1,0:T(8,128)(2,1)} %rest_0_.3, bf16[4096,2048]{1,0:T(8,128)(2,1)} %collective-permute-done.l1.rest_1_, ...), custom_call_target="tpu_custom_call", output_to_operand_aliasing={{}: (8, {})} | custom-call | flops 27917287424 | bytes 54525952 | tf_op jit(solution)/shard_map/pallas_call | solution.py:309
  1038.7 25.2 %collective-permute-start.12 = (bf16[512,512]{1,0:T(8,128)(2,1)S(1)}, bf16[512,512]{1,0:T(8,128)(2,1)S(1)}, u32[]{:S(2)}, u32[]{:S(2)}) collective-permute-start(bf16[512,512]{1,0:T(8,128)(2,1)S(1)} %slice.48), channel_id=1, source_target_pairs={{0,4},{1,5},{2,6},{3,7}} | collective-permute-start | bytes 1572872 | tf_op jit(solution)/shard_map/ppermute | solution.py:282
  1066.0 18.3 %collective-permute-start.13 = (bf16[512,256]{1,0:T(8,128)(2,1)S(1)}, bf16[512,256]{1,0:T(8,128)(2,1)S(1)}, u32[]{:S(2)}, u32[]{:S(2)}) collective-permute-start(bf16[512,256]{1,0:T(8,128)(2,1)S(1)} %slice.49), channel_id=1, source_target_pairs={{0,4},{1,5},{2,6},{3,7}} | collective-permute-start | bytes 786440 | tf_op jit(solution)/shard_map/ppermute | solution.py:282
  1084.4 3.2 collective-permute-done.11.piece
  1088.5 12.5 %collective-permute-start.14 = (bf16[256,256]{1,0:T(8,128)(2,1)S(1)}, bf16[256,256]{1,0:T(8,128)(2,1)S(1)}, u32[]{:S(2)}, u32[]{:S(2)}) collective-permute-start(bf16[256,256]{1,0:T(8,128)(2,1)S(1)} %slice.50), channel_id=1, source_target_pairs={{0,4},{1,5},{2,6},{3,7}} | collective-permute-start | bytes 393224 | tf_op jit(solution)/shard_map/ppermute | solution.py:282
  1104.3 2.8 shard_map.55.rest_1_
  (34 shorter events, 13.3 us)
Async XLA Ops:
  0.0 363.8 %collective-permute-start.1 = (bf16[4096,2048]{1,0:T(8,128)(2,1)}, bf16[4096,2048]{1,0:T(8,128)(2,1)}, u32[]{:S(2)}, u32[]{:S(2)}) collective-permute-start(bf16[4096,2048]{1,0:T(8,128)(2,1)} %rest_0_.3), channel_id=1, source_target_pairs={{0,2},{1,3},{2,0},{3,1},{4,6},{5,7},{6,4},{7,5}} | collective-permute-start | bytes 50331656 | tf_op jit(solution)/shard_map/ppermute | solution.py:287
  3.3 676.8 %collective-permute-start = (bf16[4096,2048]{1,0:T(8,128)(2,1)}, bf16[4096,2048]{1,0:T(8,128)(2,1)}, u32[]{:S(2)}, u32[]{:S(2)}) collective-permute-start(bf16[4096,2048]{1,0:T(8,128)(2,1)} %rest_0_.3), channel_id=1, source_target_pairs={{0,1},{1,0},{2,3},{3,2},{4,5},{5,4},{6,7},{7,6}} | collective-permute-start | bytes 50331656 | tf_op jit(solution)/shard_map/ppermute | solution.py:288
  363.8 319.5 %collective-permute-start.2 = (bf16[4096,2048]{1,0:T(8,128)(2,1)}, bf16[4096,2048]{1,0:T(8,128)(2,1)}, u32[]{:S(2)}, u32[]{:S(2)}) collective-permute-start(bf16[4096,2048]{1,0:T(8,128)(2,1)} %collective-permute-done.1.l2.rest_2_), channel_id=1, source_target_pairs={{0,1},{1,0},{2,3},{3,2},{4,5},{5,4},{6,7},{7,6}} | collective-permute-start | bytes 50331656 | tf_op jit(solution)/shard_map/ppermute | solution.py:289
  375.7 327.8 %collective-permute-start.5 = (bf16[4096,1024]{1,0:T(8,128)(2,1)}, bf16[4096,1024]{1,0:T(8,128)(2,1)}, u32[]{:S(2)}, u32[]{:S(2)}) collective-permute-start(bf16[4096,1024]{1,0:T(8,128)(2,1)} %slice.42), channel_id=1, source_target_pairs={{0,4},{1,5},{2,6},{3,7}} | collective-permute-start | bytes 25165832 | tf_op jit(solution)/shard_map/ppermute | solution.py:282
  382.6 294.2 %collective-permute-start.8 = (bf16[3072,512]{1,0:T(8,128)(2,1)S(1)}, bf16[3072,512]{1,0:T(8,128)(2,1)}, u32[]{:S(2)}, u32[]{:S(2)}) collective-permute-start(bf16[3072,512]{1,0:T(8,128)(2,1)S(1)} %slice.41), channel_id=1, source_target_pairs={{0,4},{1,5},{2,6},{3,7}} | collective-permute-start | bytes 9437192 | tf_op jit(solution)/shard_map/ppermute | solution.py:282
  385.5 250.3 %collective-permute-start.6 = (bf16[384,512]{1,0:T(8,128)(2,1)S(1)}, bf16[384,512]{1,0:T(8,128)(2,1)S(1)}, u32[]{:S(2)}, u32[]{:S(2)}) collective-permute-start(bf16[384,512]{1,0:T(8,128)(2,1)S(1)} %slice.39), channel_id=1, source_target_pairs={{0,4},{4,0},{1,5},{5,1},{2,6},{6,2},{3,7},{7,3}} | collective-permute-start | bytes 1179656 | tf_op jit(solution)/shard_map/ppermute | solution.py:282
  635.8 12.0 %copy-start.3 = (bf16[384,512]{1,0:T(8,128)(2,1)}, bf16[384,512]{1,0:T(8,128)(2,1)S(1)}, u32[]{:S(2)}) copy-start(bf16[384,512]{1,0:T(8,128)(2,1)S(1)} %collective-permute-done.6.rest_0_) | copy-start | bytes 1179652
  635.8 18.2 %collective-permute-start.7 = (bf16[640,512]{1,0:T(8,128)(2,1)S(1)}, bf16[640,512]{1,0:T(8,128)(2,1)S(1)}, u32[]{:S(2)}, u32[]{:S(2)}) collective-permute-start(bf16[640,512]{1,0:T(8,128)(2,1)S(1)} %slice.40), channel_id=1, source_target_pairs={{0,4},{1,5},{2,6},{3,7}} | collective-permute-start | bytes 1966088 | tf_op jit(solution)/shard_map/ppermute | solution.py:282
  654.0 0.8 copy-start.2
  654.8 185.5 %collective-permute-start.4 = (bf16[4096,1024]{1,0:T(8,128)(2,1)}, bf16[4096,1024]{1,0:T(8,128)(2,1)}, u32[]{:S(2)}, u32[]{:S(2)}) collective-permute-start(bf16[4096,1024]{1,0:T(8,128)(2,1)} %slice.43), channel_id=1, source_target_pairs={{0,4},{1,5},{2,6},{3,7}} | collective-permute-start | bytes 25165832 | tf_op jit(solution)/shard_map/ppermute | solution.py:282
  666.9 19.0 %copy-start = (s32[312]{0:T(512)S(1)}, s32[312]{0:T(512)}, u32[]{:S(2)}) copy-start(s32[312]{0:T(512)} %constant.13.clone.tab) | copy-start | bytes 3748
  676.8 253.4 %collective-permute-start.3 = (bf16[4096,512]{1,0:T(8,128)(2,1)}, bf16[4096,512]{1,0:T(8,128)(2,1)}, u32[]{:S(2)}, u32[]{:S(2)}) collective-permute-start(bf16[4096,512]{1,0:T(8,128)(2,1)} %slice.44), channel_id=1, source_target_pairs={{0,4},{1,5},{2,6},{3,7}} | collective-permute-start | bytes 12582920 | tf_op jit(solution)/shard_map/ppermute | solution.py:282
  680.1 340.0 %collective-permute-start.9 = (bf16[4096,512]{1,0:T(8,128)(2,1)}, bf16[4096,512]{1,0:T(8,128)(2,1)}, u32[]{:S(2)}, u32[]{:S(2)}) collective-permute-start(bf16[4096,512]{1,0:T(8,128)(2,1)} %slice.45), channel_id=1, source_target_pairs={{0,4},{1,5},{2,6},{3,7}} | collective-permute-start | bytes 12582920 | tf_op jit(solution)/shard_map/ppermute | solution.py:282
  683.4 381.7 %collective-permute-start.10 = (bf16[2048,512]{1,0:T(8,128)(2,1)}, bf16[2048,512]{1,0:T(8,128)(2,1)}, u32[]{:S(2)}, u32[]{:S(2)}) collective-permute-start(bf16[2048,512]{1,0:T(8,128)(2,1)} %slice.46), channel_id=1, source_target_pairs={{0,4},{1,5},{2,6},{3,7}} | collective-permute-start | bytes 6291464 | tf_op jit(solution)/shard_map/ppermute | solution.py:282
  703.5 384.0 %collective-permute-start.11 = (bf16[1024,512]{1,0:T(8,128)(2,1)}, bf16[1024,512]{1,0:T(8,128)(2,1)}, u32[]{:S(2)}, u32[]{:S(2)}) collective-permute-start(bf16[1024,512]{1,0:T(8,128)(2,1)} %slice.47), channel_id=1, source_target_pairs={{0,4},{1,5},{2,6},{3,7}} | collective-permute-start | bytes 3145736 | tf_op jit(solution)/shard_map/ppermute | solution.py:282
  869.8 77.9 %copy-start.1 = (s32[120]{0:T(128)S(1)}, s32[120]{0:T(128)}, u32[]{:S(2)}) copy-start(s32[120]{0:T(128)} %constant.14.clone.tab) | copy-start | bytes 1444
  1038.7 64.5 %collective-permute-start.12 = (bf16[512,512]{1,0:T(8,128)(2,1)S(1)}, bf16[512,512]{1,0:T(8,128)(2,1)S(1)}, u32[]{:S(2)}, u32[]{:S(2)}) collective-permute-start(bf16[512,512]{1,0:T(8,128)(2,1)S(1)} %slice.48), channel_id=1, source_target_pairs={{0,4},{1,5},{2,6},{3,7}} | collective-permute-start | bytes 1572872 | tf_op jit(solution)/shard_map/ppermute | solution.py:282
  1066.0 38.2 %collective-permute-start.13 = (bf16[512,256]{1,0:T(8,128)(2,1)S(1)}, bf16[512,256]{1,0:T(8,128)(2,1)S(1)}, u32[]{:S(2)}, u32[]{:S(2)}) collective-permute-start(bf16[512,256]{1,0:T(8,128)(2,1)S(1)} %slice.49), channel_id=1, source_target_pairs={{0,4},{1,5},{2,6},{3,7}} | collective-permute-start | bytes 786440 | tf_op jit(solution)/shard_map/ppermute | solution.py:282
  1088.5 18.6 %collective-permute-start.14 = (bf16[256,256]{1,0:T(8,128)(2,1)S(1)}, bf16[256,256]{1,0:T(8,128)(2,1)S(1)}, u32[]{:S(2)}, u32[]{:S(2)}) collective-permute-start(bf16[256,256]{1,0:T(8,128)(2,1)S(1)} %slice.50), channel_id=1, source_target_pairs={{0,4},{1,5},{2,6},{3,7}} | collective-permute-start | bytes 393224 | tf_op jit(solution)/shard_map/ppermute | solution.py:282
  1101.9 5.8 collective-permute-start.15

commit v5 on v4

--- a/solution.py
+++ b/solution.py
@@ -14,7 +14,7 @@
 NBUF = 6
 FIELDS = 6
 WIDTHS = (512, 1024, 1024, 512, 512)
-FIRST = (384, 640)
+FIRST = (288, 736)
 TAIL = (2048, 1024, 512, 512)
 LAST = ((256, (512,)), (256, (256, 256)))
 KEEP = 1024
@@ -71,11 +71,13 @@
             b_loc.at[pl.ds(k * KB, KB), pl.ds(src0, width)], bv.at[pl.ds(slot * KB, KB), :], bsem.at[slot])
 
     def b_recv_start(k):
-        for ref, cut in zip(pieces, cuts):
+        for i, (ref, cut) in enumerate(zip(pieces, cuts)):
             lo, hi = max(k * KB, cut), min((k + 1) * KB, cut + ref.shape[0])
             if lo < hi:
-                pltpu.make_async_copy(
-                    ref.at[pl.ds(lo - cut, hi - lo), :], bv.at[pl.ds(lo, hi - lo), :], bsem.at[k]).start()
+                @pl.when(lax.rem(col, 2) == i - cuts.index(cut) if cuts.count(cut) > 1 else True)
+                def _():
+                    pltpu.make_async_copy(
+                        ref.at[pl.ds(lo - cut, hi - lo), :], bv.at[pl.ds(lo, hi - lo), :], bsem.at[k]).start()
 
     def o_copy(r, slot):
         return pltpu.make_async_copy(
@@ -247,6 +249,7 @@
     x_swap = [(0, 2), (1, 3), (2, 0), (3, 1)]
     core_swap = [(0, 1), (1, 0), (2, 3), (3, 2)]
     n_first = len(FIRST) + 1
+    n_cols = mesh.shape['col']
     hbm = pl.BlockSpec(memory_space=pltpu.HBM)
     vmem = pl.BlockSpec(memory_space=pltpu.VMEM)
     smem = pl.BlockSpec(memory_space=pltpu.SMEM)
@@ -279,6 +282,10 @@
             r, h, c, w = boxes[j]
             piece = source[r:r + h, c:c + w]
             piece, source = lax.optimization_barrier((piece, source))
+            if j == 1:
+                for core in range(2):
+                    recv.append(lax.ppermute(piece, ('row', 'col'), [(c, c + n_cols) for c in range(core, n_cols, 2)]))
+                return source
             recv.append(lax.ppermute(piece, 'row', [(0, 1), (1, 0)] if j == 0 else [(0, 1)]))
             return source
 
@@ -355,10 +362,10 @@
                     source = send(i, source)
                 part, keep = chunk([], (), None, tail0, 0, tail_w, diag_counts, diag_tab)
                 x, part, keep = lax.optimization_barrier((x, part, keep))
-            pieces, cuts = (recv[:n_first], tuple(cuts0)) if j == 0 else ([recv[n_first - 1 + j]], (0,))
+            pieces, cuts = (recv[:n_first + 1], tuple(cuts0[:2] + cuts0[1:])) if j == 0 else ([recv[n_first + j]], (0,))
             x = chunk(pieces, cuts, x, starts[j], starts[j], width, off_counts, off_tab)
         x, part = lax.optimization_barrier((x, part))
-        for piece, (k0, kw, c, w) in zip(recv[n_main:], boxes[n_main:]):
+        for piece, (k0, kw, c, w) in zip(recv[n_main + 1:], boxes[n_main:]):
             final = k0 + kw == half
             done = tail(keep, piece, part, x if final else None, k0, kw, c - tail0, w)
             part, x = (part, done) if final else (done, x)

time: 1110 us -> 1120 us (level)
    ppermute x0 -> x2, waiting for transfers between devices: none -> 16.6 us  [send(): lax.ppermute(piece, ('row', 'col'), [(c, c + n_cols) for c in range(core,...]
    ppermute x13 -> x12, waiting for transfers between devices: 470 us -> 460 us  [send(): lax.ppermute(piece, 'row', [(0, 1), (1, 0)] if j == 0 else [(0, 1)])]
    ppermute x13 -> x12, starting transfers between devices: 103 us -> 98.4 us  [send(): lax.ppermute(piece, 'row', [(0, 1), (1, 0)] if j == 0 else [(0, 1)])]
  transfers between devices with their start and end apart: 16 -> 17, of which waited for: 10 -> 8; matrix products, arithmetic and copies ran while one was open for 3% -> 3% of each run, Pallas kernels for 12% -> 12%
where the time goes in v5:
time: 1120 us
  waiting for transfers between devices  838 us (75%)
  Pallas kernels  132 us (12%)
  starting transfers between devices  107 us (10%)
  local copies, waits for them, and re-layouts  38.5 us (3%)
    ppermute x12, waiting for transfers between devices, send(): lax.ppermute(piece, 'row', [(0, 1), (1, 0)] if j == 0 else [(0, 1)])  460 us
    ppermute x1, waiting for transfers between devices, product(): lx = lax.ppermute(l_block, 'col', x_swap)  361 us
    pallas_call x6, Pallas kernels, chunk(): pl.pallas_call(functools.partial(chunk_kernel, half, depth, src0, dst0, w...  129 us
    ppermute x12, starting transfers between devices, send(): lax.ppermute(piece, 'row', [(0, 1), (1, 0)] if j == 0 else [(0, 1)])  98.4 us
    slice x13, local copies, waits for them, and re-layouts, send(): piece = source[r:r + h, c:c + w]  37.6 us
  transfers between devices with their start and end apart: 17, of which 8 were waited for; matrix products, arithmetic and copies ran while one was open for 3% of the time, Pallas kernels for 12%

profile of v5, /device:TPU:0, one launch (start us, length us, event | category | flops | bytes accessed | tf_op | source)
XLA Modules:
  0.0 1115.5 jit_solution(11658677342610503184)
XLA Ops:
  0.0 3.3 collective-permute-start.1
  3.3 360.5 %collective-permute-done.1.l2.rest_2_ = bf16[4096,2048]{1,0:T(8,128)(2,1)} collective-permute-done((bf16[4096,2048]{1,0:T(8,128)(2,1)}, bf16[4096,2048]{1,0:T(8,128)(2,1)}, u32[]{:S(2)}, u32[]{:S(2)}) %collective-permute-start.1) | collective-permute-done | bytes 16777248 | tf_op jit(solution)/shard_map/ppermute | solution.py:294
  368.1 7.6 slice.42
  375.7 6.9 collective-permute-start.5
  382.6 2.9 collective-permute-start.9
  385.5 248.2 %collective-permute-done.6.rest_0_ = bf16[288,512]{1,0:T(8,128)(2,1)S(1)} collective-permute-done((bf16[288,512]{1,0:T(8,128)(2,1)S(1)}, bf16[288,512]{1,0:T(8,128)(2,1)S(1)}, u32[]{:S(2)}, u32[]{:S(2)}) %collective-permute-start.6) | collective-permute-done | bytes 294944 | tf_op jit(solution)/shard_map/ppermute | solution.py:289
  633.7 4.4 collective-permute-start.7
  638.1 16.6 %collective-permute-done.7.rest_1_ = bf16[736,512]{1,0:T(8,128)(2,1)S(1)} collective-permute-done((bf16[736,512]{1,0:T(8,128)(2,1)S(1)}, bf16[736,512]{1,0:T(8,128)(2,1)S(1)}, u32[]{:S(2)}, u32[]{:S(2)}) %collective-permute-start.7) | collective-permute-done | bytes 753696 | tf_op jit(solution)/shard_map/ppermute | solution.py:287
  655.4 7.6 slice.43
  663.9 7.7 collective-permute-start.4
  671.6 4.4 slice.44
  676.0 4.5 slice.45
  680.5 3.1 slice.46
  683.5 2.3 slice.47
  685.9 3.3 collective-permute-start.3
  689.2 3.3 collective-permute-start.10
  692.5 2.6 collective-permute-start.11
  695.0 17.5 %shard_map.46.rest_1_ = bf16[4096,4096]{1,0:T(8,128)(2,1)} custom-call(s32[312]{0:T(512)S(1)} %copy-done, s32[2]{0:T(128)S(1)} %pad_add_fusion.info, bf16[4096,2048]{1,0:T(8,128)(2,1)} %rest_0_.3, bf16[4096,2048]{1,0:T(8,128)(2,1)} %collective-permute-done.l1.rest_1_, bf16[4096,2048]{1,0:T(8,128)(2,1)} %collective-permute-done.1.l2.rest_2_, ...), custom_call_target="tpu_custom_call" | custom-call | flops 27917287424 | bytes 54525952 | tf_op jit(solution)/shard_map/pallas_call | solution.py:316
  712.6 14.6 %collective-permute-start.12 = (bf16[1024,512]{1,0:T(8,128)(2,1)}, bf16[1024,512]{1,0:T(8,128)(2,1)}, u32[]{:S(2)}, u32[]{:S(2)}) collective-permute-start(bf16[1024,512]{1,0:T(8,128)(2,1)} %slice.47), channel_id=1, source_target_pairs={{0,4},{1,5},{2,6},{3,7}} | collective-permute-start | bytes 3145736 | tf_op jit(solution)/shard_map/ppermute | solution.py:289
  727.1 29.4 %shard_map.47.rest_1_ = bf16[4096,4096]{1,0:T(8,128)(2,1)} custom-call(s32[312]{0:T(512)S(1)} %copy-done, s32[2]{0:T(128)S(1)} %pad_add_fusion.info, bf16[4096,2048]{1,0:T(8,128)(2,1)} %rest_0_.3, bf16[4096,2048]{1,0:T(8,128)(2,1)} %collective-permute-done.l1.rest_1_, ...), custom_call_target="tpu_custom_call", output_to_operand_aliasing={{}: (8, {})} | custom-call | flops 55834574848 | bytes 54525952 | tf_op jit(solution)/shard_map/pallas_call | solution.py:316
  756.6 92.9 %collective-permute-done.4.rest_0_ = bf16[4096,1024]{1,0:T(8,128)(2,1)} collective-permute-done((bf16[4096,1024]{1,0:T(8,128)(2,1)}, bf16[4096,1024]{1,0:T(8,128)(2,1)}, u32[]{:S(2)}, u32[]{:S(2)}) %collective-permute-start.4) | collective-permute-done | bytes 8388640 | tf_op jit(solution)/shard_map/ppermute | solution.py:289
  849.4 29.4 %shard_map.48.rest_1_ = bf16[4096,4096]{1,0:T(8,128)(2,1)} custom-call(s32[312]{0:T(512)S(1)} %copy-done, s32[2]{0:T(128)S(1)} %pad_add_fusion.info, bf16[4096,2048]{1,0:T(8,128)(2,1)} %rest_0_.3, bf16[4096,2048]{1,0:T(8,128)(2,1)} %collective-permute-done.l1.rest_1_, ...), custom_call_target="tpu_custom_call", output_to_operand_aliasing={{}: (8, {})} | custom-call | flops 55834574848 | bytes 54525952 | tf_op jit(solution)/shard_map/pallas_call | solution.py:316
  878.9 60.4 %collective-permute-done.3.rest_0_ = bf16[4096,512]{1,0:T(8,128)(2,1)} collective-permute-done((bf16[4096,512]{1,0:T(8,128)(2,1)}, bf16[4096,512]{1,0:T(8,128)(2,1)}, u32[]{:S(2)}, u32[]{:S(2)}) %collective-permute-start.3) | collective-permute-done | bytes 4194336 | tf_op jit(solution)/shard_map/ppermute | solution.py:289
  939.3 17.5 %shard_map.49.rest_1_ = bf16[4096,4096]{1,0:T(8,128)(2,1)} custom-call(s32[312]{0:T(512)S(1)} %copy-done, s32[2]{0:T(128)S(1)} %pad_add_fusion.info, bf16[4096,2048]{1,0:T(8,128)(2,1)} %rest_0_.3, bf16[4096,2048]{1,0:T(8,128)(2,1)} %collective-permute-done.l1.rest_1_, ...), custom_call_target="tpu_custom_call", output_to_operand_aliasing={{}: (8, {})} | custom-call | flops 27917287424 | bytes 54525952 | tf_op jit(solution)/shard_map/pallas_call | solution.py:316
  956.8 17.8 %shard_map.50 = (f32[4096,512]{1,0:T(8,128)S(1)}, bf16[4096,1024]{1,0:T(8,128)(2,1)S(1)}) custom-call(s32[120]{0:T(128)S(1)} %copy-done.1, s32[2]{0:T(128)S(1)} %pad_add_fusion.info, bf16[4096,2048]{1,0:T(8,128)(2,1)} %rest_0_.3, bf16[4096,2048]{1,0:T(8,128)(2,1)} %collective-permute-done.l1.rest_1_, bf16[4096,2048]{1,0:T(8,128)(2,1)} %collective-permute-done.1.l2.rest_2_, ...), custom_call_target="tpu_custom_call" | custom-call | flops 10737418240 | bytes 20971520 | tf_op jit(solution)/shard_map/pallas_call | solution.py:316
  974.6 54.6 %collective-permute-done.10.rest_0_ = bf16[4096,512]{1,0:T(8,128)(2,1)} collective-permute-done((bf16[4096,512]{1,0:T(8,128)(2,1)}, bf16[4096,512]{1,0:T(8,128)(2,1)}, u32[]{:S(2)}, u32[]{:S(2)}) %collective-permute-start.10) | collective-permute-done | bytes 4194336 | tf_op jit(solution)/shard_map/ppermute | solution.py:289
  1029.2 17.5 %shard_map.51.rest_1_ = bf16[4096,4096]{1,0:T(8,128)(2,1)} custom-call(s32[312]{0:T(512)S(1)} %copy-done, s32[2]{0:T(128)S(1)} %pad_add_fusion.info, bf16[4096,2048]{1,0:T(8,128)(2,1)} %rest_0_.3, bf16[4096,2048]{1,0:T(8,128)(2,1)} %collective-permute-done.l1.rest_1_, ...), custom_call_target="tpu_custom_call", output_to_operand_aliasing={{}: (8, {})} | custom-call | flops 27917287424 | bytes 54525952 | tf_op jit(solution)/shard_map/pallas_call | solution.py:316
  1047.8 25.2 %collective-permute-start.13 = (bf16[512,512]{1,0:T(8,128)(2,1)S(1)}, bf16[512,512]{1,0:T(8,128)(2,1)S(1)}, u32[]{:S(2)}, u32[]{:S(2)}) collective-permute-start(bf16[512,512]{1,0:T(8,128)(2,1)S(1)} %slice.48), channel_id=1, source_target_pairs={{0,4},{1,5},{2,6},{3,7}} | collective-permute-start | bytes 1572872 | tf_op jit(solution)/shard_map/ppermute | solution.py:289
  1075.2 18.3 %collective-permute-start.14 = (bf16[512,256]{1,0:T(8,128)(2,1)S(1)}, bf16[512,256]{1,0:T(8,128)(2,1)S(1)}, u32[]{:S(2)}, u32[]{:S(2)}) collective-permute-start(bf16[512,256]{1,0:T(8,128)(2,1)S(1)} %slice.49), channel_id=1, source_target_pairs={{0,4},{1,5},{2,6},{3,7}} | collective-permute-start | bytes 786440 | tf_op jit(solution)/shard_map/ppermute | solution.py:289
  1093.5 3.2 collective-permute-done.12.piece
  1097.6 12.5 %collective-permute-start.15 = (bf16[256,256]{1,0:T(8,128)(2,1)S(1)}, bf16[256,256]{1,0:T(8,128)(2,1)S(1)}, u32[]{:S(2)}, u32[]{:S(2)}) collective-permute-start(bf16[256,256]{1,0:T(8,128)(2,1)S(1)} %slice.50), channel_id=1, source_target_pairs={{0,4},{1,5},{2,6},{3,7}} | collective-permute-start | bytes 393224 | tf_op jit(solution)/shard_map/ppermute | solution.py:289
  1112.4 2.8 shard_map.55.rest_1_
  (38 shorter events, 12.5 us)
Async XLA Ops:
  0.0 363.8 %collective-permute-start.1 = (bf16[4096,2048]{1,0:T(8,128)(2,1)}, bf16[4096,2048]{1,0:T(8,128)(2,1)}, u32[]{:S(2)}, u32[]{:S(2)}) collective-permute-start(bf16[4096,2048]{1,0:T(8,128)(2,1)} %rest_0_.3), channel_id=1, source_target_pairs={{0,2},{1,3},{2,0},{3,1},{4,6},{5,7},{6,4},{7,5}} | collective-permute-start | bytes 50331656 | tf_op jit(solution)/shard_map/ppermute | solution.py:294
  3.3 685.9 %collective-permute-start = (bf16[4096,2048]{1,0:T(8,128)(2,1)}, bf16[4096,2048]{1,0:T(8,128)(2,1)}, u32[]{:S(2)}, u32[]{:S(2)}) collective-permute-start(bf16[4096,2048]{1,0:T(8,128)(2,1)} %rest_0_.3), channel_id=1, source_target_pairs={{0,1},{1,0},{2,3},{3,2},{4,5},{5,4},{6,7},{7,6}} | collective-permute-start | bytes 50331656 | tf_op jit(solution)/shard_map/ppermute | solution.py:295
  363.8 328.6 %collective-permute-start.2 = (bf16[4096,2048]{1,0:T(8,128)(2,1)}, bf16[4096,2048]{1,0:T(8,128)(2,1)}, u32[]{:S(2)}, u32[]{:S(2)}) collective-permute-start(bf16[4096,2048]{1,0:T(8,128)(2,1)} %collective-permute-done.1.l2.rest_2_), channel_id=1, source_target_pairs={{0,1},{1,0},{2,3},{3,2},{4,5},{5,4},{6,7},{7,6}} | collective-permute-start | bytes 50331656 | tf_op jit(solution)/shard_map/ppermute | solution.py:296
  375.7 336.8 %collective-permute-start.5 = (bf16[4096,1024]{1,0:T(8,128)(2,1)}, bf16[4096,1024]{1,0:T(8,128)(2,1)}, u32[]{:S(2)}, u32[]{:S(2)}) collective-permute-start(bf16[4096,1024]{1,0:T(8,128)(2,1)} %slice.42), channel_id=1, source_target_pairs={{0,4},{1,5},{2,6},{3,7}} | collective-permute-start | bytes 25165832 | tf_op jit(solution)/shard_map/ppermute | solution.py:289
  382.6 303.3 %collective-permute-start.9 = (bf16[3072,512]{1,0:T(8,128)(2,1)S(1)}, bf16[3072,512]{1,0:T(8,128)(2,1)}, u32[]{:S(2)}, u32[]{:S(2)}) collective-permute-start(bf16[3072,512]{1,0:T(8,128)(2,1)S(1)} %slice.41), channel_id=1, source_target_pairs={{0,4},{1,5},{2,6},{3,7}} | collective-permute-start | bytes 9437192 | tf_op jit(solution)/shard_map/ppermute | solution.py:289
  385.5 248.2 %collective-permute-start.6 = (bf16[288,512]{1,0:T(8,128)(2,1)S(1)}, bf16[288,512]{1,0:T(8,128)(2,1)S(1)}, u32[]{:S(2)}, u32[]{:S(2)}) collective-permute-start(bf16[288,512]{1,0:T(8,128)(2,1)S(1)} %slice.39), channel_id=1, source_target_pairs={{0,4},{4,0},{1,5},{5,1},{2,6},{6,2},{3,7},{7,3}} | collective-permute-start | bytes 884744 | tf_op jit(solution)/shard_map/ppermute | solution.py:289
  633.7 29.3 %copy-start.4 = (bf16[288,512]{1,0:T(8,128)(2,1)}, bf16[288,512]{1,0:T(8,128)(2,1)S(1)}, u32[]{:S(2)}) copy-start(bf16[288,512]{1,0:T(8,128)(2,1)S(1)} %collective-permute-done.6.rest_0_) | copy-start | bytes 884740
  633.7 21.0 %collective-permute-start.7 = (bf16[736,512]{1,0:T(8,128)(2,1)S(1)}, bf16[736,512]{1,0:T(8,128)(2,1)S(1)}, u32[]{:S(2)}, u32[]{:S(2)}) collective-permute-start(bf16[736,512]{1,0:T(8,128)(2,1)S(1)} %slice.40), channel_id=1, source_target_pairs={{0,4},{2,6}} | collective-permute-start | bytes 2261000 | tf_op jit(solution)/shard_map/ppermute | solution.py:287
  654.7 8.3 copy-start.2
  654.7 8.3 collective-permute-start.8
  663.0 0.9 copy-start.3
  663.9 185.5 %collective-permute-start.4 = (bf16[4096,1024]{1,0:T(8,128)(2,1)}, bf16[4096,1024]{1,0:T(8,128)(2,1)}, u32[]{:S(2)}, u32[]{:S(2)}) collective-permute-start(bf16[4096,1024]{1,0:T(8,128)(2,1)} %slice.43), channel_id=1, source_target_pairs={{0,4},{1,5},{2,6},{3,7}} | collective-permute-start | bytes 25165832 | tf_op jit(solution)/shard_map/ppermute | solution.py:289
  676.0 19.0 %copy-start = (s32[312]{0:T(512)S(1)}, s32[312]{0:T(512)}, u32[]{:S(2)}) copy-start(s32[312]{0:T(512)} %constant.13.clone.tab) | copy-start | bytes 3748
  685.9 253.4 %collective-permute-start.3 = (bf16[4096,512]{1,0:T(8,128)(2,1)}, bf16[4096,512]{1,0:T(8,128)(2,1)}, u32[]{:S(2)}, u32[]{:S(2)}) collective-permute-start(bf16[4096,512]{1,0:T(8,128)(2,1)} %slice.44), channel_id=1, source_target_pairs={{0,4},{1,5},{2,6},{3,7}} | collective-permute-start | bytes 12582920 | tf_op jit(solution)/shard_map/ppermute | solution.py:289
  689.2 340.0 %collective-permute-start.10 = (bf16[4096,512]{1,0:T(8,128)(2,1)}, bf16[4096,512]{1,0:T(8,128)(2,1)}, u32[]{:S(2)}, u32[]{:S(2)}) collective-permute-start(bf16[4096,512]{1,0:T(8,128)(2,1)} %slice.45), channel_id=1, source_target_pairs={{0,4},{1,5},{2,6},{3,7}} | collective-permute-start | bytes 12582920 | tf_op jit(solution)/shard_map/ppermute | solution.py:289
  692.5 381.7 %collective-permute-start.11 = (bf16[2048,512]{1,0:T(8,128)(2,1)}, bf16[2048,512]{1,0:T(8,128)(2,1)}, u32[]{:S(2)}, u32[]{:S(2)}) collective-permute-start(bf16[2048,512]{1,0:T(8,128)(2,1)} %slice.46), channel_id=1, source_target_pairs={{0,4},{1,5},{2,6},{3,7}} | collective-permute-start | bytes 6291464 | tf_op jit(solution)/shard_map/ppermute | solution.py:289
  712.6 384.1 %collective-permute-start.12 = (bf16[1024,512]{1,0:T(8,128)(2,1)}, bf16[1024,512]{1,0:T(8,128)(2,1)}, u32[]{:S(2)}, u32[]{:S(2)}) collective-permute-start(bf16[1024,512]{1,0:T(8,128)(2,1)} %slice.47), channel_id=1, source_target_pairs={{0,4},{1,5},{2,6},{3,7}} | collective-permute-start | bytes 3145736 | tf_op jit(solution)/shard_map/ppermute | solution.py:289
  878.9 77.9 %copy-start.1 = (s32[120]{0:T(128)S(1)}, s32[120]{0:T(128)}, u32[]{:S(2)}) copy-start(s32[120]{0:T(128)} %constant.14.clone.tab) | copy-start | bytes 1444
  1047.8 64.5 %collective-permute-start.13 = (bf16[512,512]{1,0:T(8,128)(2,1)S(1)}, bf16[512,512]{1,0:T(8,128)(2,1)S(1)}, u32[]{:S(2)}, u32[]{:S(2)}) collective-permute-start(bf16[512,512]{1,0:T(8,128)(2,1)S(1)} %slice.48), channel_id=1, source_target_pairs={{0,4},{1,5},{2,6},{3,7}} | collective-permute-start | bytes 1572872 | tf_op jit(solution)/shard_map/ppermute | solution.py:289
  1075.2 37.2 %collective-permute-start.14 = (bf16[512,256]{1,0:T(8,128)(2,1)S(1)}, bf16[512,256]{1,0:T(8,128)(2,1)S(1)}, u32[]{:S(2)}, u32[]{:S(2)}) collective-permute-start(bf16[512,256]{1,0:T(8,128)(2,1)S(1)} %slice.49), channel_id=1, source_target_pairs={{0,4},{1,5},{2,6},{3,7}} | collective-permute-start | bytes 786440 | tf_op jit(solution)/shard_map/ppermute | solution.py:289
  1097.6 17.6 %collective-permute-start.15 = (bf16[256,256]{1,0:T(8,128)(2,1)S(1)}, bf16[256,256]{1,0:T(8,128)(2,1)S(1)}, u32[]{:S(2)}, u32[]{:S(2)}) collective-permute-start(bf16[256,256]{1,0:T(8,128)(2,1)S(1)} %slice.50), channel_id=1, source_target_pairs={{0,4},{1,5},{2,6},{3,7}} | collective-permute-start | bytes 393224 | tf_op jit(solution)/shard_map/ppermute | solution.py:289
  1111.0 4.2 collective-permute-start.16

commit v6 on v4

--- a/solution.py
+++ b/solution.py
@@ -14,7 +14,7 @@
 NBUF = 6
 FIELDS = 6
 WIDTHS = (512, 1024, 1024, 512, 512)
-FIRST = (384, 640)
+FIRST = (288, 736)
 TAIL = (2048, 1024, 512, 512)
 LAST = ((256, (512,)), (256, (256, 256)))
 KEEP = 1024
@@ -161,6 +161,15 @@
             keep_copy(l0).wait()
 
 
+def first_kernel(b_loc, out, sem):
+    copy = pltpu.make_async_copy(b_loc.at[pl.ds(0, out.shape[0]), pl.ds(0, out.shape[1])], out, sem)
+
+    @pl.when(lax.axis_index('row') == 0)
+    def _():
+        copy.start()
+        copy.wait()
+
+
 def tail_kernel(half, depth, k0, kw, src0, dst0, width, final, early, part, piece, *rest):
     row, col = lax.axis_index('row'), lax.axis_index('col')
     tiles = half // TM
@@ -277,7 +286,14 @@
 
         def send(j, source):
             r, h, c, w = boxes[j]
-            piece = source[r:r + h, c:c + w]
+            if j == 0:
+                piece = pl.pallas_call(
+                    first_kernel, out_shape=pltpu.VMEM((h, w), dtype), in_specs=[hbm], out_specs=vmem,
+                    scratch_shapes=[pltpu.SemaphoreType.DMA],
+                    compiler_params=pltpu.CompilerParams(vmem_limit_bytes=2**20), name="first",
+                )(in_hbm(source))
+            else:
+                piece = source[r:r + h, c:c + w]
             piece, source = lax.optimization_barrier((piece, source))
             recv.append(lax.ppermute(piece, 'row', [(0, 1), (1, 0)] if j == 0 else [(0, 1)]))
             return source

time: 1110 us -> 1110 us (level)
    slice x13 -> x12, local copies, waits for them, and re-layouts: 37.6 us -> 36.6 us  [send(): piece = source[r:r + h, c:c + w]]
where the time goes in v6:
time: 1110 us
  waiting for transfers between devices  830 us (75%)
  Pallas kernels  133 us (12%)
  starting transfers between devices  106 us (10%)
  local copies, waits for them, and re-layouts  37.5 us (3%)
    ppermute x13, waiting for transfers between devices, send(): lax.ppermute(piece, 'row', [(0, 1), (1, 0)] if j == 0 else [(0, 1)])  470 us
    ppermute x1, waiting for transfers between devices, product(): lx = lax.ppermute(l_block, 'col', x_swap)  361 us
    pallas_call x6, Pallas kernels, chunk(): pl.pallas_call(functools.partial(chunk_kernel, half, depth, src0, dst0, w...  129 us
    ppermute x13, starting transfers between devices, send(): lax.ppermute(piece, 'row', [(0, 1), (1, 0)] if j == 0 else [(0, 1)])  102 us
    slice x12, local copies, waits for them, and re-layouts, send(): piece = source[r:r + h, c:c + w]  36.6 us
  transfers between devices with their start and end apart: 16, of which 10 were waited for; matrix products, arithmetic and copies ran while one was open for 3% of the time, Pallas kernels for 12%

profile of v6, /device:TPU:0, one launch (start us, length us, event | category | flops | bytes accessed | tf_op | source)
XLA Modules:
  0.0 1107.0 jit_solution(9625247888410109536)
XLA Ops:
  0.0 3.3 collective-permute-start.1
  3.3 360.5 %collective-permute-done.1.l2.rest_2_ = bf16[4096,2048]{1,0:T(8,128)(2,1)} collective-permute-done((bf16[4096,2048]{1,0:T(8,128)(2,1)}, bf16[4096,2048]{1,0:T(8,128)(2,1)}, u32[]{:S(2)}, u32[]{:S(2)}) %collective-permute-start.1) | collective-permute-done | bytes 16777248 | tf_op jit(solution)/shard_map/ppermute | solution.py:303
  368.1 7.6 slice.38
  375.7 5.9 collective-permute-start.5
  381.6 2.9 collective-permute-start.8
  384.5 248.2 %collective-permute-done.6.rest_0_ = bf16[288,512]{1,0:T(8,128)(2,1)S(1)} collective-permute-done((bf16[288,512]{1,0:T(8,128)(2,1)S(1)}, bf16[288,512]{1,0:T(8,128)(2,1)S(1)}, u32[]{:S(2)}, u32[]{:S(2)}) %collective-permute-start.6) | collective-permute-done | bytes 294944 | tf_op jit(solution)/shard_map/ppermute | solution.py:298
  632.7 4.4 collective-permute-start.7
  637.1 7.6 slice.39
  644.8 8.2 collective-permute-done.7.rest_1_
  653.9 7.7 collective-permute-start.4
  661.5 4.4 slice.40
  666.0 4.5 slice.41
  670.4 3.0 slice.42
  673.5 2.3 slice.43
  675.9 3.3 collective-permute-start.3
  679.2 3.3 collective-permute-start.9
  682.4 2.6 collective-permute-start.10
  685.0 17.5 %shard_map.46.rest_1_ = bf16[4096,4096]{1,0:T(8,128)(2,1)} custom-call(s32[312]{0:T(512)S(1)} %copy-done, s32[2]{0:T(128)S(1)} %pad_add_fusion.info, bf16[4096,2048]{1,0:T(8,128)(2,1)} %rest_0_.3, bf16[4096,2048]{1,0:T(8,128)(2,1)} %collective-permute-done.l1.rest_1_, bf16[4096,2048]{1,0:T(8,128)(2,1)} %collective-permute-done.1.l2.rest_2_, ...), custom_call_target="tpu_custom_call" | custom-call | flops 27917287424 | bytes 54525952 | tf_op jit(solution)/shard_map/pallas_call | solution.py:325
  702.5 15.1 %collective-permute-start.11 = (bf16[1024,512]{1,0:T(8,128)(2,1)}, bf16[1024,512]{1,0:T(8,128)(2,1)}, u32[]{:S(2)}, u32[]{:S(2)}) collective-permute-start(bf16[1024,512]{1,0:T(8,128)(2,1)} %slice.43), channel_id=1, source_target_pairs={{0,4},{1,5},{2,6},{3,7}} | collective-permute-start | bytes 3145736 | tf_op jit(solution)/shard_map/ppermute | solution.py:298
  717.7 29.4 %shard_map.47.rest_1_ = bf16[4096,4096]{1,0:T(8,128)(2,1)} custom-call(s32[312]{0:T(512)S(1)} %copy-done, s32[2]{0:T(128)S(1)} %pad_add_fusion.info, bf16[4096,2048]{1,0:T(8,128)(2,1)} %rest_0_.3, bf16[4096,2048]{1,0:T(8,128)(2,1)} %collective-permute-done.l1.rest_1_, ...), custom_call_target="tpu_custom_call", output_to_operand_aliasing={{}: (8, {})} | custom-call | flops 55834574848 | bytes 54525952 | tf_op jit(solution)/shard_map/pallas_call | solution.py:325
  747.1 92.3 %collective-permute-done.4.rest_0_ = bf16[4096,1024]{1,0:T(8,128)(2,1)} collective-permute-done((bf16[4096,1024]{1,0:T(8,128)(2,1)}, bf16[4096,1024]{1,0:T(8,128)(2,1)}, u32[]{:S(2)}, u32[]{:S(2)}) %collective-permute-start.4) | collective-permute-done | bytes 8388640 | tf_op jit(solution)/shard_map/ppermute | solution.py:298
  839.4 29.4 %shard_map.48.rest_1_ = bf16[4096,4096]{1,0:T(8,128)(2,1)} custom-call(s32[312]{0:T(512)S(1)} %copy-done, s32[2]{0:T(128)S(1)} %pad_add_fusion.info, bf16[4096,2048]{1,0:T(8,128)(2,1)} %rest_0_.3, bf16[4096,2048]{1,0:T(8,128)(2,1)} %collective-permute-done.l1.rest_1_, ...), custom_call_target="tpu_custom_call", output_to_operand_aliasing={{}: (8, {})} | custom-call | flops 55834574848 | bytes 54525952 | tf_op jit(solution)/shard_map/pallas_call | solution.py:325
  868.8 60.4 %collective-permute-done.3.rest_0_ = bf16[4096,512]{1,0:T(8,128)(2,1)} collective-permute-done((bf16[4096,512]{1,0:T(8,128)(2,1)}, bf16[4096,512]{1,0:T(8,128)(2,1)}, u32[]{:S(2)}, u32[]{:S(2)}) %collective-permute-start.3) | collective-permute-done | bytes 4194336 | tf_op jit(solution)/shard_map/ppermute | solution.py:298
  929.3 17.5 %shard_map.49.rest_1_ = bf16[4096,4096]{1,0:T(8,128)(2,1)} custom-call(s32[312]{0:T(512)S(1)} %copy-done, s32[2]{0:T(128)S(1)} %pad_add_fusion.info, bf16[4096,2048]{1,0:T(8,128)(2,1)} %rest_0_.3, bf16[4096,2048]{1,0:T(8,128)(2,1)} %collective-permute-done.l1.rest_1_, ...), custom_call_target="tpu_custom_call", output_to_operand_aliasing={{}: (8, {})} | custom-call | flops 27917287424 | bytes 54525952 | tf_op jit(solution)/shard_map/pallas_call | solution.py:325
  946.8 17.8 %shard_map.50 = (f32[4096,512]{1,0:T(8,128)S(1)}, bf16[4096,1024]{1,0:T(8,128)(2,1)S(1)}) custom-call(s32[120]{0:T(128)S(1)} %copy-done.1, s32[2]{0:T(128)S(1)} %pad_add_fusion.info, bf16[4096,2048]{1,0:T(8,128)(2,1)} %rest_0_.3, bf16[4096,2048]{1,0:T(8,128)(2,1)} %collective-permute-done.l1.rest_1_, bf16[4096,2048]{1,0:T(8,128)(2,1)} %collective-permute-done.1.l2.rest_2_, ...), custom_call_target="tpu_custom_call" | custom-call | flops 10737418240 | bytes 20971520 | tf_op jit(solution)/shard_map/pallas_call | solution.py:325
  964.6 54.6 %collective-permute-done.9.rest_0_ = bf16[4096,512]{1,0:T(8,128)(2,1)} collective-permute-done((bf16[4096,512]{1,0:T(8,128)(2,1)}, bf16[4096,512]{1,0:T(8,128)(2,1)}, u32[]{:S(2)}, u32[]{:S(2)}) %collective-permute-start.9) | collective-permute-done | bytes 4194336 | tf_op jit(solution)/shard_map/ppermute | solution.py:298
  1019.1 17.5 %shard_map.51.rest_1_ = bf16[4096,4096]{1,0:T(8,128)(2,1)} custom-call(s32[312]{0:T(512)S(1)} %copy-done, s32[2]{0:T(128)S(1)} %pad_add_fusion.info, bf16[4096,2048]{1,0:T(8,128)(2,1)} %rest_0_.3, bf16[4096,2048]{1,0:T(8,128)(2,1)} %collective-permute-done.l1.rest_1_, ...), custom_call_target="tpu_custom_call", output_to_operand_aliasing={{}: (8, {})} | custom-call | flops 27917287424 | bytes 54525952 | tf_op jit(solution)/shard_map/pallas_call | solution.py:325
  1037.7 25.2 %collective-permute-start.12 = (bf16[512,512]{1,0:T(8,128)(2,1)S(1)}, bf16[512,512]{1,0:T(8,128)(2,1)S(1)}, u32[]{:S(2)}, u32[]{:S(2)}) collective-permute-start(bf16[512,512]{1,0:T(8,128)(2,1)S(1)} %slice.44), channel_id=1, source_target_pairs={{0,4},{1,5},{2,6},{3,7}} | collective-permute-start | bytes 1572872 | tf_op jit(solution)/shard_map/ppermute | solution.py:298
  1065.1 18.3 %collective-permute-start.13 = (bf16[512,256]{1,0:T(8,128)(2,1)S(1)}, bf16[512,256]{1,0:T(8,128)(2,1)S(1)}, u32[]{:S(2)}, u32[]{:S(2)}) collective-permute-start(bf16[512,256]{1,0:T(8,128)(2,1)S(1)} %slice.45), channel_id=1, source_target_pairs={{0,4},{1,5},{2,6},{3,7}} | collective-permute-start | bytes 786440 | tf_op jit(solution)/shard_map/ppermute | solution.py:298
  1083.4 3.2 collective-permute-done.11.piece
  1087.5 12.5 %collective-permute-start.14 = (bf16[256,256]{1,0:T(8,128)(2,1)S(1)}, bf16[256,256]{1,0:T(8,128)(2,1)S(1)}, u32[]{:S(2)}, u32[]{:S(2)}) collective-permute-start(bf16[256,256]{1,0:T(8,128)(2,1)S(1)} %slice.46), channel_id=1, source_target_pairs={{0,4},{1,5},{2,6},{3,7}} | collective-permute-start | bytes 393224 | tf_op jit(solution)/shard_map/ppermute | solution.py:298
  1103.3 2.8 shard_map.55.rest_1_
  (34 shorter events, 13.3 us)
Async XLA Ops:
  0.0 363.8 %collective-permute-start.1 = (bf16[4096,2048]{1,0:T(8,128)(2,1)}, bf16[4096,2048]{1,0:T(8,128)(2,1)}, u32[]{:S(2)}, u32[]{:S(2)}) collective-permute-start(bf16[4096,2048]{1,0:T(8,128)(2,1)} %rest_0_.3), channel_id=1, source_target_pairs={{0,2},{1,3},{2,0},{3,1},{4,6},{5,7},{6,4},{7,5}} | collective-permute-start | bytes 50331656 | tf_op jit(solution)/shard_map/ppermute | solution.py:303
  3.3 675.8 %collective-permute-start = (bf16[4096,2048]{1,0:T(8,128)(2,1)}, bf16[4096,2048]{1,0:T(8,128)(2,1)}, u32[]{:S(2)}, u32[]{:S(2)}) collective-permute-start(bf16[4096,2048]{1,0:T(8,128)(2,1)} %rest_0_.3), channel_id=1, source_target_pairs={{0,1},{1,0},{2,3},{3,2},{4,5},{5,4},{6,7},{7,6}} | collective-permute-start | bytes 50331656 | tf_op jit(solution)/shard_map/ppermute | solution.py:304
  363.8 318.6 %collective-permute-start.2 = (bf16[4096,2048]{1,0:T(8,128)(2,1)}, bf16[4096,2048]{1,0:T(8,128)(2,1)}, u32[]{:S(2)}, u32[]{:S(2)}) collective-permute-start(bf16[4096,2048]{1,0:T(8,128)(2,1)} %collective-permute-done.1.l2.rest_2_), channel_id=1, source_target_pairs={{0,1},{1,0},{2,3},{3,2},{4,5},{5,4},{6,7},{7,6}} | collective-permute-start | bytes 50331656 | tf_op jit(solution)/shard_map/ppermute | solution.py:305
  375.7 326.8 %collective-permute-start.5 = (bf16[4096,1024]{1,0:T(8,128)(2,1)}, bf16[4096,1024]{1,0:T(8,128)(2,1)}, u32[]{:S(2)}, u32[]{:S(2)}) collective-permute-start(bf16[4096,1024]{1,0:T(8,128)(2,1)} %slice.38), channel_id=1, source_target_pairs={{0,4},{1,5},{2,6},{3,7}} | collective-permute-start | bytes 25165832 | tf_op jit(solution)/shard_map/ppermute | solution.py:298
  381.6 294.2 %collective-permute-start.8 = (bf16[3072,512]{1,0:T(8,128)(2,1)S(1)}, bf16[3072,512]{1,0:T(8,128)(2,1)}, u32[]{:S(2)}, u32[]{:S(2)}) collective-permute-start(bf16[3072,512]{1,0:T(8,128)(2,1)S(1)} %slice.37), channel_id=1, source_target_pairs={{0,4},{1,5},{2,6},{3,7}} | collective-permute-start | bytes 9437192 | tf_op jit(solution)/shard_map/ppermute | solution.py:298
  384.5 248.2 %collective-permute-start.6 = (bf16[288,512]{1,0:T(8,128)(2,1)S(1)}, bf16[288,512]{1,0:T(8,128)(2,1)S(1)}, u32[]{:S(2)}, u32[]{:S(2)}) collective-permute-start(bf16[288,512]{1,0:T(8,128)(2,1)S(1)} %first.1), channel_id=1, source_target_pairs={{0,4},{4,0},{1,5},{5,1},{2,6},{6,2},{3,7},{7,3}} | collective-permute-start | bytes 884744 | tf_op jit(solution)/shard_map/ppermute | solution.py:298
  632.7 28.8 %copy-start.3 = (bf16[288,512]{1,0:T(8,128)(2,1)}, bf16[288,512]{1,0:T(8,128)(2,1)S(1)}, u32[]{:S(2)}) copy-start(bf16[288,512]{1,0:T(8,128)(2,1)S(1)} %collective-permute-done.6.rest_0_) | copy-start | bytes 884740
  632.7 20.3 %collective-permute-start.7 = (bf16[736,512]{1,0:T(8,128)(2,1)S(1)}, bf16[736,512]{1,0:T(8,128)(2,1)S(1)}, u32[]{:S(2)}, u32[]{:S(2)}) collective-permute-start(bf16[736,512]{1,0:T(8,128)(2,1)S(1)} %slice.36), channel_id=1, source_target_pairs={{0,4},{1,5},{2,6},{3,7}} | collective-permute-start | bytes 2261000 | tf_op jit(solution)/shard_map/ppermute | solution.py:298
  653.0 0.9 copy-start.2
  653.9 185.5 %collective-permute-start.4 = (bf16[4096,1024]{1,0:T(8,128)(2,1)}, bf16[4096,1024]{1,0:T(8,128)(2,1)}, u32[]{:S(2)}, u32[]{:S(2)}) collective-permute-start(bf16[4096,1024]{1,0:T(8,128)(2,1)} %slice.39), channel_id=1, source_target_pairs={{0,4},{1,5},{2,6},{3,7}} | collective-permute-start | bytes 25165832 | tf_op jit(solution)/shard_map/ppermute | solution.py:298
  666.0 19.0 %copy-start = (s32[312]{0:T(512)S(1)}, s32[312]{0:T(512)}, u32[]{:S(2)}) copy-start(s32[312]{0:T(512)} %constant.13.clone.tab) | copy-start | bytes 3748
  675.9 253.4 %collective-permute-start.3 = (bf16[4096,512]{1,0:T(8,128)(2,1)}, bf16[4096,512]{1,0:T(8,128)(2,1)}, u32[]{:S(2)}, u32[]{:S(2)}) collective-permute-start(bf16[4096,512]{1,0:T(8,128)(2,1)} %slice.40), channel_id=1, source_target_pairs={{0,4},{1,5},{2,6},{3,7}} | collective-permute-start | bytes 12582920 | tf_op jit(solution)/shard_map/ppermute | solution.py:298
  679.2 340.0 %collective-permute-start.9 = (bf16[4096,512]{1,0:T(8,128)(2,1)}, bf16[4096,512]{1,0:T(8,128)(2,1)}, u32[]{:S(2)}, u32[]{:S(2)}) collective-permute-start(bf16[4096,512]{1,0:T(8,128)(2,1)} %slice.41), channel_id=1, source_target_pairs={{0,4},{1,5},{2,6},{3,7}} | collective-permute-start | bytes 12582920 | tf_op jit(solution)/shard_map/ppermute | solution.py:298
  682.4 381.7 %collective-permute-start.10 = (bf16[2048,512]{1,0:T(8,128)(2,1)}, bf16[2048,512]{1,0:T(8,128)(2,1)}, u32[]{:S(2)}, u32[]{:S(2)}) collective-permute-start(bf16[2048,512]{1,0:T(8,128)(2,1)} %slice.42), channel_id=1, source_target_pairs={{0,4},{1,5},{2,6},{3,7}} | collective-permute-start | bytes 6291464 | tf_op jit(solution)/shard_map/ppermute | solution.py:298
  702.5 384.0 %collective-permute-start.11 = (bf16[1024,512]{1,0:T(8,128)(2,1)}, bf16[1024,512]{1,0:T(8,128)(2,1)}, u32[]{:S(2)}, u32[]{:S(2)}) collective-permute-start(bf16[1024,512]{1,0:T(8,128)(2,1)} %slice.43), channel_id=1, source_target_pairs={{0,4},{1,5},{2,6},{3,7}} | collective-permute-start | bytes 3145736 | tf_op jit(solution)/shard_map/ppermute | solution.py:298
  868.8 77.9 %copy-start.1 = (s32[120]{0:T(128)S(1)}, s32[120]{0:T(128)}, u32[]{:S(2)}) copy-start(s32[120]{0:T(128)} %constant.14.clone.tab) | copy-start | bytes 1444
  1037.7 64.5 %collective-permute-start.12 = (bf16[512,512]{1,0:T(8,128)(2,1)S(1)}, bf16[512,512]{1,0:T(8,128)(2,1)S(1)}, u32[]{:S(2)}, u32[]{:S(2)}) collective-permute-start(bf16[512,512]{1,0:T(8,128)(2,1)S(1)} %slice.44), channel_id=1, source_target_pairs={{0,4},{1,5},{2,6},{3,7}} | collective-permute-start | bytes 1572872 | tf_op jit(solution)/shard_map/ppermute | solution.py:298
  1065.1 38.2 %collective-permute-start.13 = (bf16[512,256]{1,0:T(8,128)(2,1)S(1)}, bf16[512,256]{1,0:T(8,128)(2,1)S(1)}, u32[]{:S(2)}, u32[]{:S(2)}) collective-permute-start(bf16[512,256]{1,0:T(8,128)(2,1)S(1)} %slice.45), channel_id=1, source_target_pairs={{0,4},{1,5},{2,6},{3,7}} | collective-permute-start | bytes 786440 | tf_op jit(solution)/shard_map/ppermute | solution.py:298
  1087.5 18.6 %collective-permute-start.14 = (bf16[256,256]{1,0:T(8,128)(2,1)S(1)}, bf16[256,256]{1,0:T(8,128)(2,1)S(1)}, u32[]{:S(2)}, u32[]{:S(2)}) collective-permute-start(bf16[256,256]{1,0:T(8,128)(2,1)S(1)} %slice.46), channel_id=1, source_target_pairs={{0,4},{1,5},{2,6},{3,7}} | collective-permute-start | bytes 393224 | tf_op jit(solution)/shard_map/ppermute | solution.py:298
  1101.0 5.8 collective-permute-start.15

commit v7 on v6

--- a/solution.py
+++ b/solution.py
@@ -17,6 +17,7 @@
 FIRST = (288, 736)
 TAIL = (2048, 1024, 512, 512)
 LAST = ((256, (512,)), (256, (256, 256)))
+FINE = 512
 KEEP = 1024
 DOT = functools.partial(jnp.dot, preferred_element_type=jnp.float32)
 
@@ -172,7 +173,8 @@
 
 def tail_kernel(half, depth, k0, kw, src0, dst0, width, final, early, part, piece, *rest):
     row, col = lax.axis_index('row'), lax.axis_index('col')
-    tiles = half // TM
+    tm = FINE if final else TM
+    tiles = half // tm
     kept = k0 >= half - KEEP
     if final:
         keep, (out, ov, osem) = rest[0], rest[-3:]
@@ -185,7 +187,7 @@
     def l_copy(ref, t):
         slot = lax.rem(t, 2)
         return pltpu.make_async_copy(
-            ref.at[pl.ds(t * TM, TM), pl.ds(k0 % depth, kw)], lv.at[slot], lsem.at[slot])
+            ref.at[pl.ds(t * tm, tm), pl.ds(k0 % depth, kw)], lv.at[slot], lsem.at[slot])
 
     def l_start(t):
         for i, ref in enumerate(l_refs):
@@ -195,7 +197,7 @@
 
     def o_copy(t, c=src0):
         return pltpu.make_async_copy(
-            ov.at[t], out.at[pl.ds(t * TM, TM), pl.ds(dst0 + c, width)], osem.at[t])
+            ov.at[t], out.at[pl.ds(t * tm, tm), pl.ds(dst0 + c, width)], osem.at[t])
 
     def put(t, rows, total):
         if final:
@@ -215,7 +217,7 @@
         right = piece if kept else bv
 
         def add(t, _):
-            rows = pl.ds(pl.multiple_of(t * TM, TM), TM)
+            rows = pl.ds(pl.multiple_of(t * tm, tm), tm)
             if kept:
                 tile = keep[rows, pl.ds(k0 - (half - KEEP), kw)]
             else:
@@ -241,7 +243,7 @@
         def _():
             for c in range(0, part.shape[1], width):
                 def move(t, _):
-                    rows = pl.ds(pl.multiple_of(t * TM, TM), TM)
+                    rows = pl.ds(pl.multiple_of(t * tm, tm), tm)
                     ov[t] = part[rows, pl.ds(c, width)].astype(ov.dtype)
                     o_copy(t, c).start()
                     return 0
@@ -343,7 +345,7 @@
                 operands.append(x)
                 specs.append(hbm)
                 out, out_spec = jax.ShapeDtypeStruct(x.shape, x.dtype), hbm
-                scratch = [pltpu.VMEM((half // TM, TM, width), dtype), pltpu.SemaphoreType.DMA((half // TM,))]
+                scratch = [pltpu.VMEM((half // FINE, FINE, width), dtype), pltpu.SemaphoreType.DMA((half // FINE,))]
                 need += 2 * half * width
             else:
                 out, out_spec = pltpu.VMEM(part.shape, part.dtype), vmem

time: 1110 us -> 1110 us (level)
  no operation moved by 1% of the time
where the time goes in v7:
time: 1110 us
  waiting for transfers between devices  830 us (75%)
  Pallas kernels  133 us (12%)
  starting transfers between devices  106 us (10%)
  local copies, waits for them, and re-layouts  37.5 us (3%)
    ppermute x13, waiting for transfers between devices, send(): lax.ppermute(piece, 'row', [(0, 1), (1, 0)] if j == 0 else [(0, 1)])  470 us
    ppermute x1, waiting for transfers between devices, product(): lx = lax.ppermute(l_block, 'col', x_swap)  361 us
    pallas_call x6, Pallas kernels, chunk(): pl.pallas_call(functools.partial(chunk_kernel, half, depth, src0, dst0, w...  129 us
    ppermute x13, starting transfers between devices, send(): lax.ppermute(piece, 'row', [(0, 1), (1, 0)] if j == 0 else [(0, 1)])  102 us
    slice x12, local copies, waits for them, and re-layouts, send(): piece = source[r:r + h, c:c + w]  36.6 us
  transfers between devices with their start and end apart: 16, of which 10 were waited for; matrix products, arithmetic and copies ran while one was open for 3% of the time, Pallas kernels for 12%

profile of v7, /device:TPU:0, one launch (start us, length us, event | category | flops | bytes accessed | tf_op | source)
XLA Modules:
  0.0 1107.0 jit_solution(5787877051284954449)
XLA Ops:
  0.0 3.3 collective-permute-start.1
  3.3 360.5 %collective-permute-done.1.l2.rest_2_ = bf16[4096,2048]{1,0:T(8,128)(2,1)} collective-permute-done((bf16[4096,2048]{1,0:T(8,128)(2,1)}, bf16[4096,2048]{1,0:T(8,128)(2,1)}, u32[]{:S(2)}, u32[]{:S(2)}) %collective-permute-start.1) | collective-permute-done | bytes 16777248 | tf_op jit(solution)/shard_map/ppermute | solution.py:305
  368.1 7.6 slice.38
  375.7 5.9 collective-permute-start.5
  381.6 2.9 collective-permute-start.8
  384.5 248.2 %collective-permute-done.6.rest_0_ = bf16[288,512]{1,0:T(8,128)(2,1)S(1)} collective-permute-done((bf16[288,512]{1,0:T(8,128)(2,1)S(1)}, bf16[288,512]{1,0:T(8,128)(2,1)S(1)}, u32[]{:S(2)}, u32[]{:S(2)}) %collective-permute-start.6) | collective-permute-done | bytes 294944 | tf_op jit(solution)/shard_map/ppermute | solution.py:300
  632.7 4.4 collective-permute-start.7
  637.1 7.6 slice.39
  644.8 8.2 collective-permute-done.7.rest_1_
  653.9 7.7 collective-permute-start.4
  661.5 4.4 slice.40
  666.0 4.5 slice.41
  670.4 3.0 slice.42
  673.5 2.3 slice.43
  675.9 3.3 collective-permute-start.3
  679.2 3.3 collective-permute-start.9
  682.4 2.6 collective-permute-start.10
  685.0 17.5 %shard_map.46.rest_1_ = bf16[4096,4096]{1,0:T(8,128)(2,1)} custom-call(s32[312]{0:T(512)S(1)} %copy-done, s32[2]{0:T(128)S(1)} %pad_add_fusion.info, bf16[4096,2048]{1,0:T(8,128)(2,1)} %rest_0_.3, bf16[4096,2048]{1,0:T(8,128)(2,1)} %collective-permute-done.l1.rest_1_, bf16[4096,2048]{1,0:T(8,128)(2,1)} %collective-permute-done.1.l2.rest_2_, ...), custom_call_target="tpu_custom_call" | custom-call | flops 27917287424 | bytes 54525952 | tf_op jit(solution)/shard_map/pallas_call | solution.py:327
  702.5 15.1 %collective-permute-start.11 = (bf16[1024,512]{1,0:T(8,128)(2,1)}, bf16[1024,512]{1,0:T(8,128)(2,1)}, u32[]{:S(2)}, u32[]{:S(2)}) collective-permute-start(bf16[1024,512]{1,0:T(8,128)(2,1)} %slice.43), channel_id=1, source_target_pairs={{0,4},{1,5},{2,6},{3,7}} | collective-permute-start | bytes 3145736 | tf_op jit(solution)/shard_map/ppermute | solution.py:300
  717.7 29.4 %shard_map.47.rest_1_ = bf16[4096,4096]{1,0:T(8,128)(2,1)} custom-call(s32[312]{0:T(512)S(1)} %copy-done, s32[2]{0:T(128)S(1)} %pad_add_fusion.info, bf16[4096,2048]{1,0:T(8,128)(2,1)} %rest_0_.3, bf16[4096,2048]{1,0:T(8,128)(2,1)} %collective-permute-done.l1.rest_1_, ...), custom_call_target="tpu_custom_call", output_to_operand_aliasing={{}: (8, {})} | custom-call | flops 55834574848 | bytes 54525952 | tf_op jit(solution)/shard_map/pallas_call | solution.py:327
  747.1 92.3 %collective-permute-done.4.rest_0_ = bf16[4096,1024]{1,0:T(8,128)(2,1)} collective-permute-done((bf16[4096,1024]{1,0:T(8,128)(2,1)}, bf16[4096,1024]{1,0:T(8,128)(2,1)}, u32[]{:S(2)}, u32[]{:S(2)}) %collective-permute-start.4) | collective-permute-done | bytes 8388640 | tf_op jit(solution)/shard_map/ppermute | solution.py:300
  839.4 29.4 %shard_map.48.rest_1_ = bf16[4096,4096]{1,0:T(8,128)(2,1)} custom-call(s32[312]{0:T(512)S(1)} %copy-done, s32[2]{0:T(128)S(1)} %pad_add_fusion.info, bf16[4096,2048]{1,0:T(8,128)(2,1)} %rest_0_.3, bf16[4096,2048]{1,0:T(8,128)(2,1)} %collective-permute-done.l1.rest_1_, ...), custom_call_target="tpu_custom_call", output_to_operand_aliasing={{}: (8, {})} | custom-call | flops 55834574848 | bytes 54525952 | tf_op jit(solution)/shard_map/pallas_call | solution.py:327
  868.8 60.4 %collective-permute-done.3.rest_0_ = bf16[4096,512]{1,0:T(8,128)(2,1)} collective-permute-done((bf16[4096,512]{1,0:T(8,128)(2,1)}, bf16[4096,512]{1,0:T(8,128)(2,1)}, u32[]{:S(2)}, u32[]{:S(2)}) %collective-permute-start.3) | collective-permute-done | bytes 4194336 | tf_op jit(solution)/shard_map/ppermute | solution.py:300
  929.3 17.5 %shard_map.49.rest_1_ = bf16[4096,4096]{1,0:T(8,128)(2,1)} custom-call(s32[312]{0:T(512)S(1)} %copy-done, s32[2]{0:T(128)S(1)} %pad_add_fusion.info, bf16[4096,2048]{1,0:T(8,128)(2,1)} %rest_0_.3, bf16[4096,2048]{1,0:T(8,128)(2,1)} %collective-permute-done.l1.rest_1_, ...), custom_call_target="tpu_custom_call", output_to_operand_aliasing={{}: (8, {})} | custom-call | flops 27917287424 | bytes 54525952 | tf_op jit(solution)/shard_map/pallas_call | solution.py:327
  946.8 17.8 %shard_map.50 = (f32[4096,512]{1,0:T(8,128)S(1)}, bf16[4096,1024]{1,0:T(8,128)(2,1)S(1)}) custom-call(s32[120]{0:T(128)S(1)} %copy-done.1, s32[2]{0:T(128)S(1)} %pad_add_fusion.info, bf16[4096,2048]{1,0:T(8,128)(2,1)} %rest_0_.3, bf16[4096,2048]{1,0:T(8,128)(2,1)} %collective-permute-done.l1.rest_1_, bf16[4096,2048]{1,0:T(8,128)(2,1)} %collective-permute-done.1.l2.rest_2_, ...), custom_call_target="tpu_custom_call" | custom-call | flops 10737418240 | bytes 20971520 | tf_op jit(solution)/shard_map/pallas_call | solution.py:327
  964.6 54.6 %collective-permute-done.9.rest_0_ = bf16[4096,512]{1,0:T(8,128)(2,1)} collective-permute-done((bf16[4096,512]{1,0:T(8,128)(2,1)}, bf16[4096,512]{1,0:T(8,128)(2,1)}, u32[]{:S(2)}, u32[]{:S(2)}) %collective-permute-start.9) | collective-permute-done | bytes 4194336 | tf_op jit(solution)/shard_map/ppermute | solution.py:300
  1019.1 17.5 %shard_map.51.rest_1_ = bf16[4096,4096]{1,0:T(8,128)(2,1)} custom-call(s32[312]{0:T(512)S(1)} %copy-done, s32[2]{0:T(128)S(1)} %pad_add_fusion.info, bf16[4096,2048]{1,0:T(8,128)(2,1)} %rest_0_.3, bf16[4096,2048]{1,0:T(8,128)(2,1)} %collective-permute-done.l1.rest_1_, ...), custom_call_target="tpu_custom_call", output_to_operand_aliasing={{}: (8, {})} | custom-call | flops 27917287424 | bytes 54525952 | tf_op jit(solution)/shard_map/pallas_call | solution.py:327
  1037.7 25.2 %collective-permute-start.12 = (bf16[512,512]{1,0:T(8,128)(2,1)S(1)}, bf16[512,512]{1,0:T(8,128)(2,1)S(1)}, u32[]{:S(2)}, u32[]{:S(2)}) collective-permute-start(bf16[512,512]{1,0:T(8,128)(2,1)S(1)} %slice.44), channel_id=1, source_target_pairs={{0,4},{1,5},{2,6},{3,7}} | collective-permute-start | bytes 1572872 | tf_op jit(solution)/shard_map/ppermute | solution.py:300
  1065.1 18.3 %collective-permute-start.13 = (bf16[512,256]{1,0:T(8,128)(2,1)S(1)}, bf16[512,256]{1,0:T(8,128)(2,1)S(1)}, u32[]{:S(2)}, u32[]{:S(2)}) collective-permute-start(bf16[512,256]{1,0:T(8,128)(2,1)S(1)} %slice.45), channel_id=1, source_target_pairs={{0,4},{1,5},{2,6},{3,7}} | collective-permute-start | bytes 786440 | tf_op jit(solution)/shard_map/ppermute | solution.py:300
  1083.4 3.2 collective-permute-done.11.piece
  1087.5 12.5 %collective-permute-start.14 = (bf16[256,256]{1,0:T(8,128)(2,1)S(1)}, bf16[256,256]{1,0:T(8,128)(2,1)S(1)}, u32[]{:S(2)}, u32[]{:S(2)}) collective-permute-start(bf16[256,256]{1,0:T(8,128)(2,1)S(1)} %slice.46), channel_id=1, source_target_pairs={{0,4},{1,5},{2,6},{3,7}} | collective-permute-start | bytes 393224 | tf_op jit(solution)/shard_map/ppermute | solution.py:300
  1103.3 2.7 shard_map.55.rest_1_
  (34 shorter events, 13.4 us)
Async XLA Ops:
  0.0 363.8 %collective-permute-start.1 = (bf16[4096,2048]{1,0:T(8,128)(2,1)}, bf16[4096,2048]{1,0:T(8,128)(2,1)}, u32[]{:S(2)}, u32[]{:S(2)}) collective-permute-start(bf16[4096,2048]{1,0:T(8,128)(2,1)} %rest_0_.3), channel_id=1, source_target_pairs={{0,2},{1,3},{2,0},{3,1},{4,6},{5,7},{6,4},{7,5}} | collective-permute-start | bytes 50331656 | tf_op jit(solution)/shard_map/ppermute | solution.py:305
  3.3 675.8 %collective-permute-start = (bf16[4096,2048]{1,0:T(8,128)(2,1)}, bf16[4096,2048]{1,0:T(8,128)(2,1)}, u32[]{:S(2)}, u32[]{:S(2)}) collective-permute-start(bf16[4096,2048]{1,0:T(8,128)(2,1)} %rest_0_.3), channel_id=1, source_target_pairs={{0,1},{1,0},{2,3},{3,2},{4,5},{5,4},{6,7},{7,6}} | collective-permute-start | bytes 50331656 | tf_op jit(solution)/shard_map/ppermute | solution.py:306
  363.8 318.6 %collective-permute-start.2 = (bf16[4096,2048]{1,0:T(8,128)(2,1)}, bf16[4096,2048]{1,0:T(8,128)(2,1)}, u32[]{:S(2)}, u32[]{:S(2)}) collective-permute-start(bf16[4096,2048]{1,0:T(8,128)(2,1)} %collective-permute-done.1.l2.rest_2_), channel_id=1, source_target_pairs={{0,1},{1,0},{2,3},{3,2},{4,5},{5,4},{6,7},{7,6}} | collective-permute-start | bytes 50331656 | tf_op jit(solution)/shard_map/ppermute | solution.py:307
  375.7 326.8 %collective-permute-start.5 = (bf16[4096,1024]{1,0:T(8,128)(2,1)}, bf16[4096,1024]{1,0:T(8,128)(2,1)}, u32[]{:S(2)}, u32[]{:S(2)}) collective-permute-start(bf16[4096,1024]{1,0:T(8,128)(2,1)} %slice.38), channel_id=1, source_target_pairs={{0,4},{1,5},{2,6},{3,7}} | collective-permute-start | bytes 25165832 | tf_op jit(solution)/shard_map/ppermute | solution.py:300
  381.6 294.2 %collective-permute-start.8 = (bf16[3072,512]{1,0:T(8,128)(2,1)S(1)}, bf16[3072,512]{1,0:T(8,128)(2,1)}, u32[]{:S(2)}, u32[]{:S(2)}) collective-permute-start(bf16[3072,512]{1,0:T(8,128)(2,1)S(1)} %slice.37), channel_id=1, source_target_pairs={{0,4},{1,5},{2,6},{3,7}} | collective-permute-start | bytes 9437192 | tf_op jit(solution)/shard_map/ppermute | solution.py:300
  384.5 248.2 %collective-permute-start.6 = (bf16[288,512]{1,0:T(8,128)(2,1)S(1)}, bf16[288,512]{1,0:T(8,128)(2,1)S(1)}, u32[]{:S(2)}, u32[]{:S(2)}) collective-permute-start(bf16[288,512]{1,0:T(8,128)(2,1)S(1)} %first.1), channel_id=1, source_target_pairs={{0,4},{4,0},{1,5},{5,1},{2,6},{6,2},{3,7},{7,3}} | collective-permute-start | bytes 884744 | tf_op jit(solution)/shard_map/ppermute | solution.py:300
  632.7 28.8 %copy-start.3 = (bf16[288,512]{1,0:T(8,128)(2,1)}, bf16[288,512]{1,0:T(8,128)(2,1)S(1)}, u32[]{:S(2)}) copy-start(bf16[288,512]{1,0:T(8,128)(2,1)S(1)} %collective-permute-done.6.rest_0_) | copy-start | bytes 884740
  632.7 20.3 %collective-permute-start.7 = (bf16[736,512]{1,0:T(8,128)(2,1)S(1)}, bf16[736,512]{1,0:T(8,128)(2,1)S(1)}, u32[]{:S(2)}, u32[]{:S(2)}) collective-permute-start(bf16[736,512]{1,0:T(8,128)(2,1)S(1)} %slice.36), channel_id=1, source_target_pairs={{0,4},{1,5},{2,6},{3,7}} | collective-permute-start | bytes 2261000 | tf_op jit(solution)/shard_map/ppermute | solution.py:300
  653.0 0.9 copy-start.2
  653.9 185.5 %collective-permute-start.4 = (bf16[4096,1024]{1,0:T(8,128)(2,1)}, bf16[4096,1024]{1,0:T(8,128)(2,1)}, u32[]{:S(2)}, u32[]{:S(2)}) collective-permute-start(bf16[4096,1024]{1,0:T(8,128)(2,1)} %slice.39), channel_id=1, source_target_pairs={{0,4},{1,5},{2,6},{3,7}} | collective-permute-start | bytes 25165832 | tf_op jit(solution)/shard_map/ppermute | solution.py:300
  666.0 19.0 %copy-start = (s32[312]{0:T(512)S(1)}, s32[312]{0:T(512)}, u32[]{:S(2)}) copy-start(s32[312]{0:T(512)} %constant.13.clone.tab) | copy-start | bytes 3748
  675.9 253.4 %collective-permute-start.3 = (bf16[4096,512]{1,0:T(8,128)(2,1)}, bf16[4096,512]{1,0:T(8,128)(2,1)}, u32[]{:S(2)}, u32[]{:S(2)}) collective-permute-start(bf16[4096,512]{1,0:T(8,128)(2,1)} %slice.40), channel_id=1, source_target_pairs={{0,4},{1,5},{2,6},{3,7}} | collective-permute-start | bytes 12582920 | tf_op jit(solution)/shard_map/ppermute | solution.py:300
  679.2 340.0 %collective-permute-start.9 = (bf16[4096,512]{1,0:T(8,128)(2,1)}, bf16[4096,512]{1,0:T(8,128)(2,1)}, u32[]{:S(2)}, u32[]{:S(2)}) collective-permute-start(bf16[4096,512]{1,0:T(8,128)(2,1)} %slice.41), channel_id=1, source_target_pairs={{0,4},{1,5},{2,6},{3,7}} | collective-permute-start | bytes 12582920 | tf_op jit(solution)/shard_map/ppermute | solution.py:300
  682.4 381.7 %collective-permute-start.10 = (bf16[2048,512]{1,0:T(8,128)(2,1)}, bf16[2048,512]{1,0:T(8,128)(2,1)}, u32[]{:S(2)}, u32[]{:S(2)}) collective-permute-start(bf16[2048,512]{1,0:T(8,128)(2,1)} %slice.42), channel_id=1, source_target_pairs={{0,4},{1,5},{2,6},{3,7}} | collective-permute-start | bytes 6291464 | tf_op jit(solution)/shard_map/ppermute | solution.py:300
  702.5 384.0 %collective-permute-start.11 = (bf16[1024,512]{1,0:T(8,128)(2,1)}, bf16[1024,512]{1,0:T(8,128)(2,1)}, u32[]{:S(2)}, u32[]{:S(2)}) collective-permute-start(bf16[1024,512]{1,0:T(8,128)(2,1)} %slice.43), channel_id=1, source_target_pairs={{0,4},{1,5},{2,6},{3,7}} | collective-permute-start | bytes 3145736 | tf_op jit(solution)/shard_map/ppermute | solution.py:300
  868.8 77.9 %copy-start.1 = (s32[120]{0:T(128)S(1)}, s32[120]{0:T(128)}, u32[]{:S(2)}) copy-start(s32[120]{0:T(128)} %constant.14.clone.tab) | copy-start | bytes 1444
  1037.7 64.5 %collective-permute-start.12 = (bf16[512,512]{1,0:T(8,128)(2,1)S(1)}, bf16[512,512]{1,0:T(8,128)(2,1)S(1)}, u32[]{:S(2)}, u32[]{:S(2)}) collective-permute-start(bf16[512,512]{1,0:T(8,128)(2,1)S(1)} %slice.44), channel_id=1, source_target_pairs={{0,4},{1,5},{2,6},{3,7}} | collective-permute-start | bytes 1572872 | tf_op jit(solution)/shard_map/ppermute | solution.py:300
  1065.1 38.2 %collective-permute-start.13 = (bf16[512,256]{1,0:T(8,128)(2,1)S(1)}, bf16[512,256]{1,0:T(8,128)(2,1)S(1)}, u32[]{:S(2)}, u32[]{:S(2)}) collective-permute-start(bf16[512,256]{1,0:T(8,128)(2,1)S(1)} %slice.45), channel_id=1, source_target_pairs={{0,4},{1,5},{2,6},{3,7}} | collective-permute-start | bytes 786440 | tf_op jit(solution)/shard_map/ppermute | solution.py:300
  1087.5 18.5 %collective-permute-start.14 = (bf16[256,256]{1,0:T(8,128)(2,1)S(1)}, bf16[256,256]{1,0:T(8,128)(2,1)S(1)}, u32[]{:S(2)}, u32[]{:S(2)}) collective-permute-start(bf16[256,256]{1,0:T(8,128)(2,1)S(1)} %slice.46), channel_id=1, source_target_pairs={{0,4},{1,5},{2,6},{3,7}} | collective-permute-start | bytes 393224 | tf_op jit(solution)/shard_map/ppermute | solution.py:300
  1101.0 5.8 collective-permute-start.15
